TPU v7x, 256 devices: a whole 4x4x8 slice. The times are simulated.
256 devices in a mesh: row: 16 (over x_lo, y, core), col: 16 (over x_hi, z).
Axes of the slice: x: 4 (x_hi: 2, x_lo: 2; x = x_hi * 2 + x_lo), y: 4, z: 8, core: 2. Of those that a mesh axis runs over, the one named last changes fastest.
Arguments:
- node_features: bfloat16 [262144, 128], P(('row', 'col')), may hold values from -6 to 6
- src_norm: float32 [262144], P(('row', 'col')), may hold values from 0.05 to 1
- dst_norm: float32 [16, 16384], P('col', 'row'), may hold values from 0.1 to 1
- tiles: bfloat16 [16, 16, 320, 128, 128], P('row', 'col'), may hold values from 0 to 0.049804688
- row_block: int32 [16, 16, 320], P('row', 'col'), may hold values from 0 to 127
- col_block: int32 [16, 16, 320], P('row', 'col'), may hold values from 0 to 127
- tile_count: int32 [16, 16], P('row', 'col'), may hold values from 40 to 320, as said below
- weight: bfloat16 [128, 128], replicated, may hold values from -0.5 to 0.5
- bias: float32 [128], replicated, may hold values from -3 to 3
Outputs:
- result: bfloat16 [16, 16384, 128], P('col', 'row')
Inputs may be any that keep to these rules, and one draw needn't show every extreme that they name: Slots at or beyond a grid cell's tile_count are ignored (their ids are 0); the live slots of one grid cell name distinct (row_block, col_block) pairs; some grid cell has all 320 slots live.
All inputs are finite; a program needn't handle non-finite values.
Results may differ from a plain program's by a relative error of at most 0.0095.
Values may be sent and summed in bfloat16 or wider, within the bound.
No kernel may reach another device: no remote copies, remote signals or barrier semaphores. Data moves between devices by JAX's collectives and lax.ppermute only.
A program may use at most 128 MiB of HBM per device.

v0:
```python
import jax
import jax.numpy as jnp
from jax import lax
from jax.sharding import Mesh
from jax.sharding import PartitionSpec as P

COL = ("col_0", "col_1")
ROW_COL = ("row", "col_0", "col_1")


def laid_out(pieces, dim):
    pieces = jnp.moveaxis(pieces, 0, dim)
    dims = pieces.shape
    return pieces.reshape(*dims[:dim], dims[dim] * dims[dim + 1], *dims[dim + 2 :])


def gather_in_order(shard, axes, turns):
    pieces = shard[None]
    for k in turns:
        pieces = lax.all_gather(pieces, axes[k], axis=0, tiled=True)
    block = [lax.axis_size(axes[k]) for k in reversed(turns)]
    pieces = pieces.reshape(*block, *shard.shape)
    turned = sorted(range(len(turns)), key=lambda place: turns[len(turns) - 1 - place])
    return pieces.transpose(*turned, *range(len(turns), pieces.ndim)).reshape(-1, *shard.shape)


def gathered_by_axis(shard, axes, turns, dim):
    return laid_out(gather_in_order(shard, axes, turns), dim)


def shards(
    node_features, src_norm, dst_norm, tiles, row_block, col_block, tile_count, weight, bias
):
    tile_size = tiles.shape[-1]
    feat_width = node_features.shape[1]
    slot_count = tiles.shape[2]
    scaled = (src_norm[:, None] * node_features.astype(jnp.float32)).astype(jnp.bfloat16)
    tile_set = tiles[0, 0]
    row_ids = row_block[0, 0]
    col_ids = col_block[0, 0]
    live_count = tile_count[0, 0]
    live_mask = jnp.arange(slot_count, dtype=jnp.int32) < live_count
    gathered = gathered_by_axis(scaled, COL, (0, 1), 0)
    blocks = gathered.reshape(-1, tile_size, feat_width)
    picked = jnp.take(blocks, col_ids, axis=0)
    products = jnp.einsum("tij,tjf->tif", tile_set, picked, preferred_element_type=jnp.float32)
    flat_prods = products.reshape(slot_count, tile_size * feat_width)
    out_rows = dst_norm.shape[1]
    dest_blocks = out_rows * lax.axis_size("row") // tile_size
    wanted = jnp.arange(dest_blocks, dtype=jnp.int32)
    onehot = ((row_ids[None, :] == wanted[:, None]) & live_mask[None, :]).astype(jnp.float32)
    summed = jnp.dot(onehot, flat_prods, preferred_element_type=jnp.float32)
    partial_sum = summed.reshape(dest_blocks * tile_size, feat_width)
    aggregate = lax.psum_scatter(
        partial_sum.astype(jnp.bfloat16), "row", scatter_dimension=0, tiled=True
    ).astype(jnp.float32)
    hidden = (dst_norm[0][:, None] * aggregate).astype(jnp.bfloat16)
    mixed = jnp.dot(hidden, weight, preferred_element_type=jnp.float32) + bias
    return jnp.maximum(mixed, 0.0).astype(jnp.bfloat16)[None]


def solution(mesh):
    torus = Mesh(mesh.devices.reshape(mesh.shape["row"], 2, 8), ("row", "col_0", "col_1"))
    in_specs = (
        P(ROW_COL, None),
        P(ROW_COL),
        P(COL, "row"),
        P("row", COL, None, None, None),
        P("row", COL, None),
        P("row", COL, None),
        P("row", COL),
        P(),
        P(),
    )
    out_specs = P(COL, "row", None)
    return jax.shard_map(
        shards, mesh=torus, in_specs=in_specs, out_specs=out_specs, check_vma=False
    )
```

profile of v0, /device:TPU:4, one launch (start us, length us, event | category | flops | bytes accessed | tf_op | source)
XLA Modules:
  0.0 221.1 jit_solution(7910911394478809684)
XLA Ops:
  6.5 0.0 copy-start
  6.5 0.0 all-gather.3.cloned.1.call-start
  6.5 1.2 multiply_convert_fusion.1
  7.7 10.3 %all-gather = bf16[2048,128]{1,0:T(8,128)(2,1)} all-gather(bf16[1024,128]{1,0:T(8,128)(2,1)S(1)} %multiply_convert_fusion.1), channel_id=2, replica_groups=mesh['row'=16,'col_0'=2,'col_1'=8] {'col_0'}, dimensions={0}, use_global_device_ids=true | all-gather | bytes 786432 | tf_op jit(solution)/shard_map/all_gather | solution.py:20
  18.0 0.0 all-gather.3.cloned.1.call-update
  18.1 0.0 reduce-scatter.2.cloned.1.call-start
  18.1 0.7 reduce.1
  18.8 0.7 reduce
  20.2 0.7 fusion.24
  20.9 55.0 %all-gather.3.cloned.1.call-done = bf16[16,1024,128]{2,1,0:T(8,128)(2,1)} async-done(((bf16[2,1024,128]{2,1,0:T(8,128)(2,1)}), bf16[16,1024,128]{2,1,0:T(8,128)(2,1)}) %all-gather.3.cloned.1.call-update) | async-done | bytes 4194320 | tf_op jit(solution)/shard_map/all_gather | solution.py:20
  75.9 4.7 %copy.15 = bf16[2,8,1024,128]{3,2,1,0:T(8,128)(2,1)} copy(bf16[2,8,1024,128]{3,2,0,1:T(8,128)(2,1)} %bitcast.28) | data formatting | bytes 8388608 | tf_op jit(solution)/shard_map/transpose | solution.py:24
  80.6 12.9 %gather_fusion = bf16[320,128,128]{2,1,0:T(8,128)(2,1)} fusion(bf16[128,128,128]{2,1,0:T(8,128)(2,1)} %bitcast.26, s32[1024]{0:T(1024)S(1)} %pad_clamp_fusion), kind=kCustom, calls=%fused_computation | custom fusion | bytes 20972800 | tf_op jit(solution)/shard_map/jit(_take)/gather | solution.py:45
  93.4 15.9 %fusion.10 = bf16[320,128,128]{1,2,0:T(8,128)(2,1)} fusion(bf16[1,1,320,128,128]{4,3,2,1,0:T(8,128)(2,1)} %param.12, bf16[320,128,128]{2,1,0:T(8,128)(2,1)} %gather_fusion, pred[320]{0:T(512)(128)(4,1)S(1)} %compare_and_fusion), kind=kOutput, calls=%fused_computation.9 | convolution fusion | flops 1347420160 | bytes 31457600 | tf_op jit(solution)/shard_map/tij,tjf->tif/dot_general | solution.py:46
  109.3 14.4 %copy.17 = bf16[320,128,128]{2,1,0:T(8,128)(2,1)} copy(bf16[320,128,128]{1,2,0:T(8,128)(2,1)} %fusion.10) | data formatting | bytes 20971520 | tf_op jit(solution)/shard_map/tij,tjf->tif/dot_general | solution.py:46
  123.7 12.7 %fusion.3 = bf16[128,16384]{1,0:T(8,128)(2,1)} fusion(bf16[40,8,128,128]{3,2,1,0:T(8,128)(2,1)} %bitcast.27, s32[320]{0:T(512)S(1)} %reduce, pred[320]{0:T(512)(128)(4,1)S(1)} %iota_compare_fusion.1), kind=kOutput, calls=%fused_computation.4 | convolution fusion | flops 1342259200 | bytes 14681664 | tf_op jit(solution)/shard_map/dot_general | solution.py:52
  136.3 0.0 copy-start.1
  136.3 0.0 copy-start.2
  136.3 7.4 %convert_element_type.25 = bf16[16384,128]{1,0:T(8,128)(2,1)} reshape(bf16[128,16384]{1,0:T(8,128)(2,1)} %fusion.3) | data formatting | bytes 8388608 | tf_op jit(solution)/shard_map/convert_element_type | solution.py:55
  143.8 0.0 reduce-scatter.2.cloned.1.call-update
  143.8 68.4 %reduce-scatter.2.cloned.1.call-done = bf16[1024,128]{1,0:T(8,128)(2,1)} async-done(((bf16[16384,128]{1,0:T(8,128)(2,1)}), bf16[1024,128]{1,0:T(8,128)(2,1)}) %reduce-scatter.2.cloned.1.call-update) | async-done | bytes 262160 | tf_op jit(solution)/shard_map/reduce_scatter | solution.py:54
  212.3 0.0 copy-done
  212.3 0.0 copy-done.1
  212.3 0.0 copy-done.2
  212.3 2.0 fusion.18
  (3 shorter events, 0.0 us)
Async XLA Ops:
  6.5 205.7 %copy-start = (bf16[128,128]{1,0:T(8,128)(2,1)S(1)}, bf16[128,128]{1,0:T(8,128)(2,1)}, u32[]{:S(2)}) copy-start(bf16[128,128]{1,0:T(8,128)(2,1)} %param.16) | copy-start | bytes 98308
  6.5 69.3 %all-gather.3.cloned.1.call-start = ((), (), s32[]{:S(2)}) async-start(), calls=%async_computation.1 | async-start | bytes 4718592 | tf_op jit(solution)/shard_map/all_gather | solution.py:20
  18.1 194.2 %reduce-scatter.2.cloned.1.call-start = ((), (), s32[]{:S(2)}) async-start(), calls=%async_computation.2 | async-start | bytes 4456448 | tf_op jit(solution)/shard_map/reduce_scatter | solution.py:54
  136.3 75.9 %copy-start.1 = (f32[1,1024]{1,0:T(1,128)S(1)}, f32[1,1024]{1,0:T(1,128)}, u32[]{:S(2)}) copy-start(f32[1,1024]{1,0:T(1,128)} %param.11) | copy-start | bytes 12292
  136.3 75.9 %copy-start.2 = (f32[128]{0:T(128)S(1)}, f32[128]{0:T(128)}, u32[]{:S(2)}) copy-start(f32[128]{0:T(128)} %param.17) | copy-start | bytes 1540
Sparse Core Ops, SparseCore 0:
  18.2 57.6 all-gather.2
  143.9 68.2 reduce-scatter.1
where the time goes:
time: 222 us; the launch traced here: 221 us
  waiting for transfers between devices  123 us (55%)
  local copies, waits for them, and re-layouts  39.4 us (18%)
  matrix products  30.5 us (14%)
  between operations  14.1 us (6%)
  blocking collectives  10.3 us (5%)
  other arithmetic  3.28 us (1%)
    reduce_scatter x1, waiting for transfers between devices, shards(): lax.psum_scatter(partial_sum.astype(jnp.bfloat16), 'row', scatter_dimensi...  68.4 us
    all_gather x1, waiting for transfers between devices, gather_in_order(): pieces = lax.all_gather(pieces, axes[k], axis=0, tiled=True)  55 us
    dot_general x1, matrix products, shards(): jnp.einsum('tij,tjf->tif', tile_set, picked, preferred_element_type=jnp.f...  15.9 us
    dot_general x1, local copies, waits for them, and re-layouts, shards(): jnp.einsum('tij,tjf->tif', tile_set, picked, preferred_element_type=jnp.f...  14.4 us
    gather x1, local copies, waits for them, and re-layouts, shards(): picked = jnp.take(blocks, col_ids, axis=0)  12.9 us
    dot_general x1, matrix products, shards(): summed = jnp.dot(onehot, flat_prods, preferred_element_type=jnp.float32)  12.7 us
    all_gather x1, blocking collectives, gather_in_order(): pieces = lax.all_gather(pieces, axes[k], axis=0, tiled=True)  10.3 us
    convert_element_type x1, local copies, waits for them, and re-layouts, shards(): partial_sum.astype(jnp.bfloat16)  7.43 us
  transfers between devices with their start and end apart: 2, of which 2 were waited for; matrix products, arithmetic and copies ran while one was open for 1% of the time, Pallas kernels for 0%

commit v1 on v0

--- a/solution.py
+++ b/solution.py
@@ -1,11 +1,15 @@
 import jax
 import jax.numpy as jnp
 from jax import lax
+from jax.experimental import pallas as pl
+from jax.experimental.pallas import tpu as pltpu
 from jax.sharding import Mesh
 from jax.sharding import PartitionSpec as P
 
 COL = ("col_0", "col_1")
 ROW_COL = ("row", "col_0", "col_1")
+CHUNK = 16
+GROUP = 4
 
 
 def laid_out(pieces, dim):
@@ -28,31 +32,82 @@
     return laid_out(gather_in_order(shard, axes, turns), dim)
 
 
+def tile_sums(
+    count_ref, row_ref, col_ref, feat_hbm, tiles_hbm, out_ref, feat, tiles, acc, tile_sem, feat_sem
+):
+    count = count_ref[0]
+    dests = out_ref.shape[0]
+    chunks = (count + CHUNK - 1) // CHUNK
+
+    def tile_copy(k):
+        span = pl.ds(pl.multiple_of(k * CHUNK, CHUNK), CHUNK)
+        return pltpu.make_async_copy(tiles_hbm.at[span], tiles.at[span], tile_sem.at[k])
+
+    feat_copy = pltpu.make_async_copy(feat_hbm, feat, feat_sem)
+    feat_copy.start()
+
+    @pl.loop(0, chunks)
+    def _(k):
+        tile_copy(k).start()
+
+    @pl.loop(0, dests, unroll=4)
+    def _(d):
+        acc[d] = jnp.zeros(acc.shape[1:], acc.dtype)
+
+    feat_copy.wait()
+
+    @pl.loop(0, chunks)
+    def _(k):
+        tile_copy(k).wait()
+        for first in range(0, CHUNK, GROUP):
+            slots = [k * CHUNK + first + u for u in range(GROUP)]
+            products = [
+                jnp.dot(tiles[t], feat[col_ref[t]], preferred_element_type=jnp.float32)
+                for t in slots
+            ]
+            for t, product in zip(slots, products):
+                acc[jnp.where(t < count, row_ref[t], dests)] += product
+
+    @pl.loop(0, dests, unroll=4)
+    def _(d):
+        out_ref[d] = acc[d].astype(out_ref.dtype)
+
+
+def block_sparse_product(count, row_ids, col_ids, blocks, tiles, dests):
+    slots, side, _ = tiles.shape
+    width = blocks.shape[-1]
+    return pl.pallas_call(
+        tile_sums,
+        out_shape=jax.ShapeDtypeStruct((dests, side, width), jnp.bfloat16),
+        in_specs=[pl.BlockSpec(memory_space=pltpu.SMEM)] * 3
+        + [pl.BlockSpec(memory_space=pl.ANY)] * 2,
+        out_specs=pl.BlockSpec(memory_space=pltpu.VMEM),
+        scratch_shapes=[
+            pltpu.VMEM(blocks.shape, jnp.bfloat16),
+            pltpu.VMEM(tiles.shape, jnp.bfloat16),
+            pltpu.VMEM((dests + 1, side, width), jnp.float32),
+            pltpu.SemaphoreType.DMA((slots // CHUNK,)),
+            pltpu.SemaphoreType.DMA,
+        ],
+        compiler_params=pltpu.CompilerParams(vmem_limit_bytes=40 * 2**20),
+        name="tile_sums",
+    )(count, row_ids, col_ids, blocks, tiles)
+
+
 def shards(
     node_features, src_norm, dst_norm, tiles, row_block, col_block, tile_count, weight, bias
 ):
     tile_size = tiles.shape[-1]
     feat_width = node_features.shape[1]
-    slot_count = tiles.shape[2]
     scaled = (src_norm[:, None] * node_features.astype(jnp.float32)).astype(jnp.bfloat16)
-    tile_set = tiles[0, 0]
-    row_ids = row_block[0, 0]
-    col_ids = col_block[0, 0]
-    live_count = tile_count[0, 0]
-    live_mask = jnp.arange(slot_count, dtype=jnp.int32) < live_count
     gathered = gathered_by_axis(scaled, COL, (0, 1), 0)
     blocks = gathered.reshape(-1, tile_size, feat_width)
-    picked = jnp.take(blocks, col_ids, axis=0)
-    products = jnp.einsum("tij,tjf->tif", tile_set, picked, preferred_element_type=jnp.float32)
-    flat_prods = products.reshape(slot_count, tile_size * feat_width)
-    out_rows = dst_norm.shape[1]
-    dest_blocks = out_rows * lax.axis_size("row") // tile_size
-    wanted = jnp.arange(dest_blocks, dtype=jnp.int32)
-    onehot = ((row_ids[None, :] == wanted[:, None]) & live_mask[None, :]).astype(jnp.float32)
-    summed = jnp.dot(onehot, flat_prods, preferred_element_type=jnp.float32)
-    partial_sum = summed.reshape(dest_blocks * tile_size, feat_width)
+    dest_blocks = dst_norm.shape[1] * lax.axis_size("row") // tile_size
+    partial_sum = block_sparse_product(
+        tile_count[0], row_block[0, 0], col_block[0, 0], blocks, tiles[0, 0], dest_blocks
+    ).reshape(dest_blocks * tile_size, feat_width)
     aggregate = lax.psum_scatter(
-        partial_sum.astype(jnp.bfloat16), "row", scatter_dimension=0, tiled=True
+        partial_sum, "row", scatter_dimension=0, tiled=True
     ).astype(jnp.float32)
     hidden = (dst_norm[0][:, None] * aggregate).astype(jnp.bfloat16)
     mixed = jnp.dot(hidden, weight, preferred_element_type=jnp.float32) + bias

time: 222 us -> 167 us (0.75)
  local copies, waits for them, and re-layouts: 39.4 us -> 4.52 us
  matrix products: 30.5 us -> 1.98 us
  Pallas kernels: 0 us -> 5.72 us
  waiting for transfers between devices: 123 us -> 127 us
    dot_general x2 -> x0, matrix products: 28.5 us -> none  [the longest x1 15.9 us: shards(): jnp.einsum('tij,tjf->tif', tile_set, picked, preferred_element_type=jnp.f...]
    dot_general x1 -> x0, local copies, waits for them, and re-layouts: 14.4 us -> none  [shards(): jnp.einsum('tij,tjf->tif', tile_set, picked, preferred_element_type=jnp.f...]
    gather x1 -> x0, local copies, waits for them, and re-layouts: 12.9 us -> none  [shards(): picked = jnp.take(blocks, col_ids, axis=0)]
    convert_element_type x1 -> x0, local copies, waits for them, and re-layouts: 7.43 us -> none  [shards(): partial_sum.astype(jnp.bfloat16)]
    pallas_call x0 -> x1, Pallas kernels: none -> 5.72 us  [block_sparse_product(): pl.pallas_call(tile_sums, out_shape=jax.ShapeDtypeStruct((dests, side, wi...]
    reduce_scatter x1, waiting for transfers between devices: 68.4 us -> 71.4 us  [shards(): lax.psum_scatter(partial_sum, 'row', scatter_dimension=0, tiled=True)]
where the time goes in v1:
time: 167 us; the launch traced here: 166 us
  waiting for transfers between devices  127 us (76%)
  between operations  14.1 us (8%)
  blocking collectives  10.3 us (6%)
  Pallas kernels  5.72 us (3%)
  local copies, waits for them, and re-layouts  4.52 us (3%)
  other arithmetic  2.56 us (2%)
  matrix products  1.98 us (1%)
    reduce_scatter x1, waiting for transfers between devices, shards(): lax.psum_scatter(partial_sum, 'row', scatter_dimension=0, tiled=True)  71.4 us
    all_gather x1, waiting for transfers between devices, gather_in_order(): pieces = lax.all_gather(pieces, axes[k], axis=0, tiled=True)  55.7 us
    all_gather x1, blocking collectives, gather_in_order(): pieces = lax.all_gather(pieces, axes[k], axis=0, tiled=True)  10.3 us
    pallas_call x1, Pallas kernels, block_sparse_product(): pl.pallas_call(tile_sums, out_shape=jax.ShapeDtypeStruct((dests, side, wi...  5.72 us
  transfers between devices with their start and end apart: 2, of which 2 were waited for; matrix products, arithmetic and copies ran while one was open for 1% of the time, Pallas kernels for 0%

profile of v1, /device:TPU:4, one launch (start us, length us, event | category | flops | bytes accessed | tf_op | source)
XLA Modules:
  0.0 166.4 jit_solution(14613870124277378208)
XLA Ops:
  6.5 0.0 copy-start
  6.5 0.0 all-gather.3.cloned.1.call-start
  6.5 1.2 multiply_convert_fusion.1
  7.7 10.3 %all-gather = bf16[2048,128]{1,0:T(8,128)(2,1)} all-gather(bf16[1024,128]{1,0:T(8,128)(2,1)S(1)} %multiply_convert_fusion.1), channel_id=2, replica_groups=mesh['row'=16,'col_0'=2,'col_1'=8] {'col_0'}, dimensions={0}, use_global_device_ids=true | all-gather | bytes 786432 | tf_op jit(solution)/shard_map/all_gather | solution.py:24
  18.0 0.0 all-gather.3.cloned.1.call-update
  18.1 0.0 reduce-scatter.2.cloned.1.call-start
  18.7 0.7 reduce.row_ref
  19.5 0.7 reduce.1.col_ref
  20.1 55.7 %all-gather.3.cloned.1.call-done = bf16[16,1024,128]{2,1,0:T(8,128)(2,1)} async-done(((bf16[2,1024,128]{2,1,0:T(8,128)(2,1)}), bf16[16,1024,128]{2,1,0:T(8,128)(2,1)}) %all-gather.3.cloned.1.call-update) | async-done | bytes 4194320 | tf_op jit(solution)/shard_map/all_gather | solution.py:24
  75.9 2.6 %copy.11 = bf16[2,8,1024,128]{3,2,1,0:T(8,128)(2,1)S(1)} copy(bf16[2,8,1024,128]{3,2,0,1:T(8,128)(2,1)} %bitcast.16) | data formatting | bytes 8388608 | tf_op jit(solution)/shard_map/transpose | solution.py:28
  78.5 5.7 %tile_sums.1 = bf16[128,128,128]{2,1,0:T(8,128)(2,1)S(1)} custom-call(s32[1]{0:T(128)} %bitcast.12.count_ref, s32[320]{0:T(512)S(1)} %reduce.row_ref, s32[320]{0:T(512)S(1)} %reduce.1.col_ref, bf16[128,128,128]{2,1,0:T(8,128)(2,1)S(1)} %bitcast.14, bf16[320,128,128]{2,1,0:T(8,128)(2,1)} %bitcast.15), custom_call_target="tpu_custom_call" | custom-call | tf_op jit(solution)/shard_map/tile_sums/pallas_call | solution.py:79
  84.2 0.0 copy-start.1
  84.2 1.9 %copy-done.1 = bf16[128,128,128]{2,1,0:T(8,128)(2,1)} copy-done((bf16[128,128,128]{2,1,0:T(8,128)(2,1)}, bf16[128,128,128]{2,1,0:T(8,128)(2,1)S(1)}, u32[]{:S(2)}) %copy-start.1) | copy-done | bytes 4194328
  86.1 0.0 copy-start.2
  86.1 0.0 copy-start.3
  86.1 0.0 reduce-scatter.2.cloned.1.call-update
  86.2 71.4 %reduce-scatter.2.cloned.1.call-done = bf16[1024,128]{1,0:T(8,128)(2,1)} async-done(((bf16[16384,128]{1,0:T(8,128)(2,1)}), bf16[1024,128]{1,0:T(8,128)(2,1)}) %reduce-scatter.2.cloned.1.call-update) | async-done | bytes 262160 | tf_op jit(solution)/shard_map/reduce_scatter | solution.py:109
  157.5 0.0 copy-done
  157.5 0.0 copy-done.2
  157.5 0.0 copy-done.3
  157.5 2.0 %fusion.2 = bf16[1,1024,128]{2,1,0:T(8,128)(2,1)} fusion(bf16[128,128]{1,0:T(8,128)(2,1)S(1)} %copy-done, bf16[1024,128]{1,0:T(8,128)(2,1)} %reduce-scatter.2.cloned.1.call-done, f32[128]{0:T(128)S(1)} %copy-done.3, f32[1024]{0:T(1024)S(1)} %bitcast.18), kind=kOutput, calls=%fused_computation.3 | convolution fusion | flops 34340864 | bytes 561664 | tf_op jit(solution)/shard_map/dot_general | solution.py:113
Async XLA Ops:
  6.5 151.0 %copy-start = (bf16[128,128]{1,0:T(8,128)(2,1)S(1)}, bf16[128,128]{1,0:T(8,128)(2,1)}, u32[]{:S(2)}) copy-start(bf16[128,128]{1,0:T(8,128)(2,1)} %param.16) | copy-start | bytes 98308
  6.5 69.3 %all-gather.3.cloned.1.call-start = ((), (), s32[]{:S(2)}) async-start(), calls=%async_computation.1 | async-start | bytes 4718592 | tf_op jit(solution)/shard_map/all_gather | solution.py:24
  18.1 139.5 %reduce-scatter.2.cloned.1.call-start = ((), (), s32[]{:S(2)}) async-start(), calls=%async_computation.2 | async-start | bytes 4456448 | tf_op jit(solution)/shard_map/reduce_scatter | solution.py:109
  84.2 1.9 %copy-start.1 = (bf16[128,128,128]{2,1,0:T(8,128)(2,1)}, bf16[128,128,128]{2,1,0:T(8,128)(2,1)S(1)}, u32[]{:S(2)}) copy-start(bf16[128,128,128]{2,1,0:T(8,128)(2,1)S(1)} %tile_sums.1) | copy-start | bytes 12582916
  86.1 71.4 %copy-start.2 = (f32[1,1024]{1,0:T(1,128)S(1)}, f32[1,1024]{1,0:T(1,128)}, u32[]{:S(2)}) copy-start(f32[1,1024]{1,0:T(1,128)} %param.11) | copy-start | bytes 12292
  86.1 71.4 %copy-start.3 = (f32[128]{0:T(128)S(1)}, f32[128]{0:T(128)}, u32[]{:S(2)}) copy-start(f32[128]{0:T(128)} %param.17) | copy-start | bytes 1540
Sparse Core Ops, SparseCore 0:
  18.2 57.6 all-gather.2
  86.3 71.1 reduce-scatter.1

commit v2 on v1

v2 whole, which is shorter than its diff:
```python
import jax
import jax.numpy as jnp
from jax import lax
from jax.experimental import pallas as pl
from jax.experimental.pallas import tpu as pltpu
from jax.sharding import Mesh
from jax.sharding import PartitionSpec as P


ROW = ("xl", "y", "core")
COL = ("xh", "z")
CHUNK = 16
GROUP = 4
BF16 = jnp.bfloat16
F32 = jnp.float32


def shifted(value, axis, by):
    n = lax.axis_size(axis)
    return lax.ppermute(value, axis, [(i, (i + by) % n) for i in range(n)])


def swapped(value, axis):
    return lax.ppermute(value, axis, [(0, 1), (1, 0)])


def gathered(own):
    half = own.shape[0] // 2
    found = {(0, 0, 0): (own, 0), (0, 0, 1): (own, half)}
    up = shifted(own, "z", 1)
    down = shifted(own, "z", -1)
    other_top = swapped(own[:half], "xh")
    other_low = swapped(own[half:], "xh")
    found[1, 0, 0] = (other_top, 0)
    found[1, 0, 1] = (other_low, 0)
    for step in (1, 2, 3):
        for dz, value in ((-step, up), (step, down)):
            found[0, dz, 0] = (value, 0)
            found[0, dz, 1] = (value, half)
            if step > 1:
                found[1, dz + (1 if dz < 0 else -1), 0] = (value, 2 * half)
        if step < 3:
            onward_up, onward_down = up, down
            if step == 1:
                onward_up = jnp.concatenate([up, other_top])
                onward_down = jnp.concatenate([down, other_top])
        else:
            onward_up = jnp.concatenate([up[:half], up[2 * half :]])
            onward_down = down[half:]
        lows = jnp.concatenate([up[half : 2 * half], down[half : 2 * half]])
        up = shifted(onward_up, "z", 1)
        down = shifted(onward_down, "z", -1)
        lows = swapped(lows, "xh")
        found[1, -step, 1] = (lows, 0)
        found[1, step, 1] = (lows, half)
    found[0, 4, 0] = (up, 0)
    found[0, 4, 1] = (down, 0)
    found[1, -3, 0] = (up, half)
    found[1, 3, 0] = (down, half)
    last = swapped(jnp.concatenate([up[:half], down[:half]]), "xh")
    found[1, 4, 0] = (last, 0)
    found[1, 4, 1] = (last, half)
    return found


def tile_sums(places, *refs):
    (place_ref, count_ref, row_ref, col_ref), refs = refs[:4], refs[4:]
    n = len(refs) - 9
    parts, tiles_hbm = refs[:n], refs[n]
    keep_a, send_a, keep_b, send_b = refs[n + 1 : n + 5]
    feat, tiles, acc, tile_sem = refs[n + 5 : n + 9]
    count = count_ref[0]
    dests = acc.shape[0] - 1
    chunks = (count + CHUNK - 1) // CHUNK
    xl, y, core, xh, z = (place_ref[i] for i in range(5))

    def tile_copy(k):
        span = pl.ds(pl.multiple_of(k * CHUNK, CHUNK), CHUNK)
        return pltpu.make_async_copy(tiles_hbm.at[span], tiles.at[span], tile_sem.at[k])

    @pl.loop(0, chunks)
    def _(k):
        tile_copy(k).start()

    for (dx, dz, half), (part, row) in places.items():
        block = ((xh ^ dx) * 8 + ((z + dz) & 7)) * 8 + half * 4
        for i in range(4):
            feat[block + i] = parts[part][row + i * 128 : row + (i + 1) * 128]

    @pl.loop(0, dests, unroll=4)
    def _(d):
        acc[d] = jnp.zeros(acc.shape[1:], acc.dtype)

    @pl.loop(0, chunks)
    def _(k):
        tile_copy(k).wait()
        for first in range(0, CHUNK, GROUP):
            slots = [k * CHUNK + first + u for u in range(GROUP)]
            products = [
                jnp.dot(tiles[t], feat[col_ref[t]], preferred_element_type=F32) for t in slots
            ]
            for t, product in zip(slots, products):
                acc[jnp.where(t < count, row_ref[t], dests)] += product

    @pl.loop(0, 2)
    def _(dx):
        @pl.loop(0, 4)
        def _(dy):
            for mine, (to_a, to_b) in ((0, (keep_a, keep_b)), (1, (send_a, send_b))):
                block = (((xl ^ dx) * 4 + ((y + dy) & 3)) * 2 + (core ^ mine)) * 8
                for i in range(4):
                    to_a[dx, dy, i] = acc[block + i].astype(BF16)
                    to_b[dy, dx, i] = acc[block + 4 + i].astype(BF16)


def block_sparse_product(place, count, row_ids, col_ids, found, tiles, dests):
    slots, side, width = tiles.shape
    parts = list({id(value): value for value, _ in found.values()}.values())
    index = {id(value): i for i, value in enumerate(parts)}
    places = {key: (index[id(value)], row) for key, (value, row) in found.items()}
    out_a = jax.ShapeDtypeStruct((2, 4, 4, side, width), BF16)
    out_b = jax.ShapeDtypeStruct((4, 2, 4, side, width), BF16)

    def kernel(*refs):
        tile_sums(places, *refs)

    return pl.pallas_call(
        kernel,
        out_shape=(out_a, out_a, out_b, out_b),
        in_specs=[pl.BlockSpec(memory_space=pltpu.SMEM)] * 4
        + [pl.BlockSpec(memory_space=pltpu.VMEM)] * len(parts)
        + [pl.BlockSpec(memory_space=pl.ANY)],
        out_specs=[pl.BlockSpec(memory_space=pltpu.VMEM)] * 4,
        scratch_shapes=[
            pltpu.VMEM((128, side, width), BF16),
            pltpu.VMEM(tiles.shape, BF16),
            pltpu.VMEM((dests + 1, side, width), F32),
            pltpu.SemaphoreType.DMA((slots // CHUNK,)),
        ],
        compiler_params=pltpu.CompilerParams(vmem_limit_bytes=40 * 2**20),
        name="tile_sums",
    )(place, count, row_ids, col_ids, *parts, tiles)


def added(*values):
    total = values[0].astype(F32)
    for value in values[1:]:
        total = total + value.astype(F32)
    return total


def scattered(keep_a, send_a, keep_b, send_b):
    got_a = swapped(send_a, "core")
    got_b = swapped(send_b, "core")
    far_a = swapped(added(keep_a[1], got_a[1]).astype(BF16), "xl")
    far_b = [shifted(added(keep_b[k], got_b[k]).astype(BF16), "y", k) for k in (1, 3, 2)]
    sum_a = added(keep_a[0], got_a[0], far_a)
    near_a = [shifted(sum_a[k].astype(BF16), "y", k) for k in (1, 3, 2)]
    sum_b = added(keep_b[0], got_b[0], *far_b)
    last_b = swapped(sum_b[1].astype(BF16), "xl")
    total_a = added(sum_a[0], *near_a)
    total_b = added(sum_b[0], last_b)
    return jnp.concatenate([total_a, total_b]).reshape(-1, keep_a.shape[-1])


def shards(
    node_features, src_norm, dst_norm, tiles, row_block, col_block, tile_count, weight, bias
):
    place = jnp.stack([lax.axis_index(a) for a in ROW + COL]).astype(jnp.int32)
    scaled = (src_norm[:, None] * node_features.astype(F32)).astype(BF16)
    found = gathered(scaled)
    dests = dst_norm.shape[1] * 16 // tiles.shape[-1]
    sums = block_sparse_product(
        place, tile_count[0], row_block[0, 0], col_block[0, 0], found, tiles[0, 0], dests
    )
    aggregate = scattered(*sums)
    hidden = (dst_norm[0][:, None] * aggregate).astype(BF16)
    mixed = jnp.dot(hidden, weight, preferred_element_type=F32) + bias
    return jnp.maximum(mixed, 0.0).astype(BF16)[None]


def solution(mesh):
    torus = Mesh(mesh.devices.reshape(2, 4, 2, 2, 8), ROW + COL)
    in_specs = (
        P(ROW + COL, None),
        P(ROW + COL),
        P(COL, ROW),
        P(ROW, COL, None, None, None),
        P(ROW, COL, None),
        P(ROW, COL, None),
        P(ROW, COL),
        P(),
        P(),
    )
    out_specs = P(COL, ROW, None)

    return jax.shard_map(
        shards, mesh=torus, in_specs=in_specs, out_specs=out_specs, check_vma=False
    )
```

time: 167 us -> 108 us (0.65)
  waiting for transfers between devices: 127 us -> 54.8 us
  starting transfers between devices: 0.04 us -> 38.8 us
  between operations: 14.1 us -> 0.88 us
  blocking collectives: 10.3 us -> 0 us
  other arithmetic: 2.56 us -> 6.61 us
  local copies, waits for them, and re-layouts: 4.52 us -> 0.94 us
  Pallas kernels: 5.72 us -> 3.76 us
    reduce_scatter x1 -> x0, waiting for transfers between devices: 71.4 us -> none  [shards(): lax.psum_scatter(partial_sum, 'row', scatter_dimension=0, tiled=True)]
    all_gather x1 -> x0, waiting for transfers between devices: 55.7 us -> none  [gather_in_order(): pieces = lax.all_gather(pieces, axes[k], axis=0, tiled=True)]
    ppermute x0 -> x24, waiting for transfers between devices: none -> 54.8 us  [the longest x14 30.7 us: shifted(): return lax.ppermute(value, axis, [(i, (i + by) % n) for i in range(n)])]
    ppermute x0 -> x24, starting transfers between devices: none -> 38.8 us  [the longest x14 26.6 us: shifted(): return lax.ppermute(value, axis, [(i, (i + by) % n) for i in range(n)])]
    all_gather x1 -> x0, blocking collectives: 10.3 us -> none  [gather_in_order(): pieces = lax.all_gather(pieces, axes[k], axis=0, tiled=True)]
    concatenate x0 -> x7, other arithmetic: none -> 3.01 us  [the longest x3 2.18 us: gathered(): lows = jnp.concatenate([up[half:2 * half], down[half:2 * half]])]
    transpose x1 -> x0, local copies, waits for them, and re-layouts: 2.58 us -> none  [gather_in_order(): pieces.transpose(*turned, *range(len(turns), pieces.ndim))]
    pallas_call x1, Pallas kernels: 5.72 us -> 3.76 us  [block_sparse_product(): pl.pallas_call(kernel, out_shape=(out_a, out_a, out_b, out_b), in_specs=[...]
  transfers between devices with their start and end apart: 2 -> 24, of which waited for: 2 -> 13; matrix products, arithmetic and copies ran while one was open for 1% -> 6% of each run, Pallas kernels for 0% -> 0%
where the time goes in v2:
time: 108 us; the launch traced here: 107 us
  waiting for transfers between devices  54.8 us (51%)
  starting transfers between devices  38.8 us (36%)
  other arithmetic  6.61 us (6%)
  Pallas kernels  3.76 us (3%)
    ppermute x14, waiting for transfers between devices, shifted(): return lax.ppermute(value, axis, [(i, (i + by) % n) for i in range(n)])  30.7 us
    ppermute x14, starting transfers between devices, shifted(): return lax.ppermute(value, axis, [(i, (i + by) % n) for i in range(n)])  26.6 us
    ppermute x10, waiting for transfers between devices, swapped(): return lax.ppermute(value, axis, [(0, 1), (1, 0)])  24.1 us
    ppermute x10, starting transfers between devices, swapped(): return lax.ppermute(value, axis, [(0, 1), (1, 0)])  12.2 us
    pallas_call x1, Pallas kernels, block_sparse_product(): pl.pallas_call(kernel, out_shape=(out_a, out_a, out_b, out_b), in_specs=[...  3.76 us
    concatenate x3, other arithmetic, gathered(): lows = jnp.concatenate([up[half:2 * half], down[half:2 * half]])  2.18 us
  transfers between devices with their start and end apart: 24, of which 13 were waited for; matrix products, arithmetic and copies ran while one was open for 6% of the time, Pallas kernels for 0%

profile of v2, /device:TPU:4, one launch (start us, length us, event | category | flops | bytes accessed | tf_op | source)
XLA Modules:
  0.0 106.7 jit_solution(14835931395677397419)
XLA Ops:
  0.0 1.2 %multiply_convert_fusion.refs_4_ = bf16[1024,128]{1,0:T(8,128)(2,1)S(1)} fusion(bf16[1024,128]{1,0:T(8,128)(2,1)} %param.9, f32[1024]{0:T(1024)} %param.10), kind=kLoop, calls=%fused_computation.16 | loop fusion | flops 393216 | bytes 528384 | tf_op jit(solution)/shard_map/convert_element_type | solution.py:170
  1.2 5.9 %collective-permute-start.3 = (bf16[1024,128]{1,0:T(8,128)(2,1)S(1)}, bf16[1024,128]{1,0:T(8,128)(2,1)S(1)}, u32[]{:S(2)}, u32[]{:S(2)}) collective-permute-start(bf16[1024,128]{1,0:T(8,128)(2,1)S(1)} %multiply_convert_fusion.refs_4_), channel_id=1, source_target_pairs={{0,7},{1,0},{2,1},{3,2},{4,3},{5,4},{6,5},{7,6},{8,15},{9,8},{10,9... | collective-permute-start | bytes 786440 | tf_op jit(solution)/shard_map/ppermute | solution.py:20
  7.1 0.0 collective-permute-start.2
  7.1 0.7 fusion.17
  7.8 0.5 collective-permute-start
  8.3 6.0 %collective-permute-done.refs_5_ = bf16[512,128]{1,0:T(8,128)(2,1)S(1)} collective-permute-done((bf16[512,128]{1,0:T(8,128)(2,1)S(1)}, bf16[512,128]{1,0:T(8,128)(2,1)S(1)}, u32[]{:S(2)}, u32[]{:S(2)}) %collective-permute-start) | collective-permute-done | bytes 131104 | tf_op jit(solution)/shard_map/ppermute | solution.py:24
  14.3 0.0 collective-permute-done.3.refs_8_
  14.3 1.8 %collective-permute-done.2.refs_7_ = bf16[1024,128]{1,0:T(8,128)(2,1)S(1)} collective-permute-done((bf16[1024,128]{1,0:T(8,128)(2,1)S(1)}, bf16[1024,128]{1,0:T(8,128)(2,1)S(1)}, u32[]{:S(2)}, u32[]{:S(2)}) %collective-permute-start.2) | collective-permute-done | bytes 262176 | tf_op jit(solution)/shard_map/ppermute | solution.py:20
  16.1 0.1 pad_maximum_fusion.1
  16.1 1.5 %collective-permute-start.6 = (bf16[1536,128]{1,0:T(8,128)(2,1)S(1)}, bf16[1536,128]{1,0:T(8,128)(2,1)S(1)}, u32[]{:S(2)}, u32[]{:S(2)}) collective-permute-start(bf16[1536,128]{1,0:T(8,128)(2,1)S(1)} %get-tuple-element.26), channel_id=1, source_target_pairs={{0,7},{1,0},{2,1},{3,2},{4,3},{5,4},{6,5},{7,6},{8,15},{9,8},{10,9... | collective-permute-start | bytes 1179656 | tf_op jit(solution)/shard_map/ppermute | solution.py:20
  17.6 0.6 collective-permute-start.5
  18.2 7.7 %collective-permute-done.6.refs_11_ = bf16[1536,128]{1,0:T(8,128)(2,1)S(1)} collective-permute-done((bf16[1536,128]{1,0:T(8,128)(2,1)S(1)}, bf16[1536,128]{1,0:T(8,128)(2,1)S(1)}, u32[]{:S(2)}, u32[]{:S(2)}) %collective-permute-start.6) | collective-permute-done | bytes 393248 | tf_op jit(solution)/shard_map/ppermute | solution.py:20
  25.9 2.3 %collective-permute-start.9 = (bf16[1536,128]{1,0:T(8,128)(2,1)S(1)}, bf16[1536,128]{1,0:T(8,128)(2,1)S(1)}, u32[]{:S(2)}, u32[]{:S(2)}) collective-permute-start(bf16[1536,128]{1,0:T(8,128)(2,1)S(1)} %collective-permute-done.6.refs_11_), channel_id=1, source_target_pairs={{0,7},{1,0},{2,1},{3,2},{4,3},{5,4},{6,5},{7,6},{8,15},{9,8},{10,9... | collective-permute-start | bytes 1179656 | tf_op jit(solution)/shard_map/ppermute | solution.py:20
  28.3 0.0 collective-permute-done.5.refs_10_
  28.3 0.0 collective-permute-start.8
  28.3 6.8 %collective-permute-done.9.refs_14_ = bf16[1536,128]{1,0:T(8,128)(2,1)S(1)} collective-permute-done((bf16[1536,128]{1,0:T(8,128)(2,1)S(1)}, bf16[1536,128]{1,0:T(8,128)(2,1)S(1)}, u32[]{:S(2)}, u32[]{:S(2)}) %collective-permute-start.9) | collective-permute-done | bytes 393248 | tf_op jit(solution)/shard_map/ppermute | solution.py:20
  35.1 3.0 %collective-permute-start.12 = (bf16[1024,128]{1,0:T(8,128)(2,1)S(1)}, bf16[1024,128]{1,0:T(8,128)(2,1)S(1)}, u32[]{:S(2)}, u32[]{:S(2)}) collective-permute-start(bf16[1024,128]{1,0:T(8,128)(2,1)S(1)} %slice.138), channel_id=1, source_target_pairs={{0,7},{1,0},{2,1},{3,2},{4,3},{5,4},{6,5},{7,6},{8,15},{9,8},{10,9... | collective-permute-start | bytes 786440 | tf_op jit(solution)/shard_map/ppermute | solution.py:20
  38.2 0.0 collective-permute-done.8.refs_13_
  38.2 0.1 collective-permute-start.11
  38.3 0.7 pad_maximum_fusion.3
  39.0 0.0 collective-permute-start.4
  39.1 0.7 pad_maximum_fusion.4
  39.8 3.5 %collective-permute-start.7 = (bf16[1024,128]{1,0:T(8,128)(2,1)}, bf16[1024,128]{1,0:T(8,128)(2,1)}, u32[]{:S(2)}, u32[]{:S(2)}) collective-permute-start(bf16[1024,128]{1,0:T(8,128)(2,1)} %pad_maximum_fusion.4), channel_id=1, source_target_pairs={{0,8},{8,0},{1,9},{9,1},{2,10},{10,2},{3,11},{11,3},{4,12},{12,4},... | collective-permute-start | bytes 786440 | tf_op jit(solution)/shard_map/ppermute | solution.py:24
  43.4 0.7 pad_maximum_fusion.5
  44.1 0.0 collective-permute-start.10
  44.1 0.0 collective-permute-done.12.refs_17_
  44.1 1.8 %collective-permute-done.11.refs_16_ = bf16[1024,128]{1,0:T(8,128)(2,1)S(1)} collective-permute-done((bf16[1024,128]{1,0:T(8,128)(2,1)S(1)}, bf16[1024,128]{1,0:T(8,128)(2,1)S(1)}, u32[]{:S(2)}, u32[]{:S(2)}) %collective-permute-start.11) | collective-permute-done | bytes 262176 | tf_op jit(solution)/shard_map/ppermute | solution.py:20
  45.9 0.7 pad_maximum_fusion.7
  46.6 1.7 %collective-permute-start.13 = (bf16[1024,128]{1,0:T(8,128)(2,1)}, bf16[1024,128]{1,0:T(8,128)(2,1)}, u32[]{:S(2)}, u32[]{:S(2)}) collective-permute-start(bf16[1024,128]{1,0:T(8,128)(2,1)} %pad_maximum_fusion.7), channel_id=1, source_target_pairs={{0,8},{8,0},{1,9},{9,1},{2,10},{10,2},{3,11},{11,3},{4,12},{12,4},... | collective-permute-start | bytes 786440 | tf_op jit(solution)/shard_map/ppermute | solution.py:24
  48.4 1.8 %collective-permute-start.1 = (bf16[512,128]{1,0:T(8,128)(2,1)}, bf16[512,128]{1,0:T(8,128)(2,1)S(1)}, u32[]{:S(2)}, u32[]{:S(2)}) collective-permute-start(bf16[512,128]{1,0:T(8,128)(2,1)} %get-tuple-element.24), channel_id=1, source_target_pairs={{0,8},{8,0},{1,9},{9,1},{2,10},{10,2},{3,11},{11,3},{4,12},{12,4},... | collective-permute-start | bytes 393224 | tf_op jit(solution)/shard_map/ppermute | solution.py:24
  50.8 0.7 reduce.refs_2_
  51.5 0.7 reduce.1.refs_3_
  52.2 0.1 stack.23.refs_0_
  52.3 12.8 %collective-permute-done.1.refs_6_ = bf16[512,128]{1,0:T(8,128)(2,1)S(1)} collective-permute-done((bf16[512,128]{1,0:T(8,128)(2,1)}, bf16[512,128]{1,0:T(8,128)(2,1)S(1)}, u32[]{:S(2)}, u32[]{:S(2)}) %collective-permute-start.1) | collective-permute-done | bytes 131104 | tf_op jit(solution)/shard_map/ppermute | solution.py:24
  65.1 0.0 collective-permute-done.4.refs_9_
  65.1 0.0 collective-permute-done.7.refs_12_
  65.1 0.0 copy-start.1
  65.1 0.0 copy-start.2
  65.1 3.8 %tile_sums.1 = (bf16[2,4,4,128,128]{4,3,2,1,0:T(8,128)(2,1)S(1)}, bf16[2,4,4,128,128]{4,3,2,1,0:T(8,128)(2,1)S(1)}, bf16[4,2,4,128,128]{4,3,2,1,0:T(8,128)(2,1)S(1)}, bf16[4,2,4,128,128]{4,3,2,1,0:T(8,128)(2,1)S(1)}) custom-call(s32[5]{0:T(128)S(1)} %stack.23.refs_0_, s32[1]{0:T(128)} %bitcast.53.refs_1_, s32[320]{0:T(512)S(1)} %reduce.refs_2_, ...), custom_call_target="tpu_custom_call" | custom-call | tf_op jit(solution)/shard_map/tile_sums/pallas_call | solution.py:127
  68.9 0.1 collective-permute-start.19
  69.0 0.5 collective-permute-start.14
  69.5 2.1 %collective-permute-done.19 = bf16[4,2,4,128,128]{4,3,2,1,0:T(8,128)(2,1)S(1)} collective-permute-done((bf16[4,2,4,128,128]{4,3,2,1,0:T(8,128)(2,1)S(1)}, bf16[4,2,4,128,128]{4,3,2,1,0:T(8,128)(2,1)S(1)}, u32[]{:S(2)}, u32[]{:S(2)}) %collective-permute-start.19) | collective-permute-done | bytes 1048608 | tf_op jit(solution)/shard_map/ppermute | solution.py:24
  71.6 0.2 fusion.7
  71.8 7.0 %collective-permute-start.20 = (bf16[2,4,128,128]{3,2,1,0:T(8,128)(2,1)S(1)}, bf16[2,4,128,128]{3,2,1,0:T(8,128)(2,1)S(1)}, u32[]{:S(2)}, u32[]{:S(2)}) collective-permute-start(bf16[2,4,128,128]{3,2,1,0:T(8,128)(2,1)S(1)} %get-tuple-element.15), channel_id=1, source_target_pairs={{0,32},{32,64},{64,96},{96,0},{1,33},{33,65},{65,97},{97,1},{2,34}... | collective-permute-start | bytes 786440 | tf_op jit(solution)/shard_map/ppermute | solution.py:20
  78.8 2.8 %collective-permute-start.21 = (bf16[2,4,128,128]{3,2,1,0:T(8,128)(2,1)S(1)}, bf16[2,4,128,128]{3,2,1,0:T(8,128)(2,1)S(1)}, u32[]{:S(2)}, u32[]{:S(2)}) collective-permute-start(bf16[2,4,128,128]{3,2,1,0:T(8,128)(2,1)S(1)} %get-tuple-element.17), channel_id=1, source_target_pairs={{0,96},{32,0},{64,32},{96,64},{1,97},{33,1},{65,33},{97,65},{2,98}... | collective-permute-start | bytes 786440 | tf_op jit(solution)/shard_map/ppermute | solution.py:20
  81.6 0.1 fusion.3
  81.8 2.0 %collective-permute-start.15 = (bf16[4,4,128,128]{3,2,1,0:T(8,128)(2,1)S(1)}, bf16[4,4,128,128]{3,2,1,0:T(8,128)(2,1)S(1)}, u32[]{:S(2)}, u32[]{:S(2)}) collective-permute-start(bf16[4,4,128,128]{3,2,1,0:T(8,128)(2,1)S(1)} %fusion.3), channel_id=1, source_target_pairs={{0,128},{128,0},{1,129},{129,1},{2,130},{130,2},{3,131},{131,3},{4... | collective-permute-start | bytes 1572872 | tf_op jit(solution)/shard_map/ppermute | solution.py:24
  83.8 1.7 %collective-permute-done.20 = bf16[2,4,128,128]{3,2,1,0:T(8,128)(2,1)S(1)} collective-permute-done((bf16[2,4,128,128]{3,2,1,0:T(8,128)(2,1)S(1)}, bf16[2,4,128,128]{3,2,1,0:T(8,128)(2,1)S(1)}, u32[]{:S(2)}, u32[]{:S(2)}) %collective-permute-start.20) | collective-permute-done | bytes 262176 | tf_op jit(solution)/shard_map/ppermute | solution.py:20
  85.5 4.8 %collective-permute-done.22 = bf16[2,4,128,128]{3,2,1,0:T(8,128)(2,1)S(1)} collective-permute-done((bf16[2,4,128,128]{3,2,1,0:T(8,128)(2,1)S(1)}, bf16[2,4,128,128]{3,2,1,0:T(8,128)(2,1)S(1)}, u32[]{:S(2)}, u32[]{:S(2)}) %collective-permute-start.22) | collective-permute-done | bytes 262176 | tf_op jit(solution)/shard_map/ppermute | solution.py:20
  90.3 0.9 collective-permute-done.21
  91.2 0.2 fusion.6
  91.4 2.0 %collective-permute-start.23 = (bf16[4,128,128]{2,1,0:T(8,128)(2,1)S(1)}, bf16[4,128,128]{2,1,0:T(8,128)(2,1)S(1)}, u32[]{:S(2)}, u32[]{:S(2)}) collective-permute-start(bf16[4,128,128]{2,1,0:T(8,128)(2,1)S(1)} %fusion.14), channel_id=1, source_target_pairs={{0,128},{128,0},{1,129},{129,1},{2,130},{130,2},{3,131},{131,3},{4... | collective-permute-start | bytes 393224 | tf_op jit(solution)/shard_map/ppermute | solution.py:24
  93.4 3.2 %collective-permute-done.15 = bf16[4,4,128,128]{3,2,1,0:T(8,128)(2,1)S(1)} collective-permute-done((bf16[4,4,128,128]{3,2,1,0:T(8,128)(2,1)S(1)}, bf16[4,4,128,128]{3,2,1,0:T(8,128)(2,1)S(1)}, u32[]{:S(2)}, u32[]{:S(2)}) %collective-permute-start.15) | collective-permute-done | bytes 524320 | tf_op jit(solution)/shard_map/ppermute | solution.py:24
  96.6 0.2 fusion.15
  96.9 0.1 collective-permute-start.16
  97.0 1.1 %collective-permute-start.18 = (bf16[4,128,128]{2,1,0:T(8,128)(2,1)S(1)}, bf16[4,128,128]{2,1,0:T(8,128)(2,1)S(1)}, u32[]{:S(2)}, u32[]{:S(2)}) collective-permute-start(bf16[4,128,128]{2,1,0:T(8,128)(2,1)S(1)} %get-tuple-element.19), channel_id=1, source_target_pairs={{0,64},{32,96},{64,0},{96,32},{1,65},{33,97},{65,1},{97,33},{2,66}... | collective-permute-start | bytes 393224 | tf_op jit(solution)/shard_map/ppermute | solution.py:20
  98.1 2.1 %collective-permute-start.17 = (bf16[4,128,128]{2,1,0:T(8,128)(2,1)S(1)}, bf16[4,128,128]{2,1,0:T(8,128)(2,1)S(1)}, u32[]{:S(2)}, u32[]{:S(2)}) collective-permute-start(bf16[4,128,128]{2,1,0:T(8,128)(2,1)S(1)} %get-tuple-element.20), channel_id=1, source_target_pairs={{0,96},{32,0},{64,32},{96,64},{1,97},{33,1},{65,33},{97,65},{2,98}... | collective-permute-start | bytes 393224 | tf_op jit(solution)/shard_map/ppermute | solution.py:20
  100.2 0.0 collective-permute-done.23
  100.3 4.3 %collective-permute-done.16 = bf16[4,128,128]{2,1,0:T(8,128)(2,1)S(1)} collective-permute-done((bf16[4,128,128]{2,1,0:T(8,128)(2,1)S(1)}, bf16[4,128,128]{2,1,0:T(8,128)(2,1)S(1)}, u32[]{:S(2)}, u32[]{:S(2)}) %collective-permute-start.16) | collective-permute-done | bytes 131104 | tf_op jit(solution)/shard_map/ppermute | solution.py:20
  104.6 0.0 collective-permute-done.18
  104.6 0.9 collective-permute-done.17
  105.5 0.1 fusion.13
  105.6 0.2 fusion.4
  105.8 0.9 fusion.2
  (22 shorter events, 0.3 us)
Async XLA Ops:
  0.0 105.8 %copy-start = (bf16[128,128]{1,0:T(8,128)(2,1)S(1)}, bf16[128,128]{1,0:T(8,128)(2,1)}, u32[]{:S(2)}) copy-start(bf16[128,128]{1,0:T(8,128)(2,1)} %param.16) | copy-start | bytes 98308
  1.2 13.1 %collective-permute-start.3 = (bf16[1024,128]{1,0:T(8,128)(2,1)S(1)}, bf16[1024,128]{1,0:T(8,128)(2,1)S(1)}, u32[]{:S(2)}, u32[]{:S(2)}) collective-permute-start(bf16[1024,128]{1,0:T(8,128)(2,1)S(1)} %multiply_convert_fusion.refs_4_), channel_id=1, source_target_pairs={{0,7},{1,0},{2,1},{3,2},{4,3},{5,4},{6,5},{7,6},{8,15},{9,8},{10,9... | collective-permute-start | bytes 786440 | tf_op jit(solution)/shard_map/ppermute | solution.py:20
  7.1 9.0 %collective-permute-start.2 = (bf16[1024,128]{1,0:T(8,128)(2,1)S(1)}, bf16[1024,128]{1,0:T(8,128)(2,1)S(1)}, u32[]{:S(2)}, u32[]{:S(2)}) collective-permute-start(bf16[1024,128]{1,0:T(8,128)(2,1)S(1)} %multiply_convert_fusion.refs_4_), channel_id=1, source_target_pairs={{0,1},{1,2},{2,3},{3,4},{4,5},{5,6},{6,7},{7,0},{8,9},{9,10},{10,1... | collective-permute-start | bytes 786440 | tf_op jit(solution)/shard_map/ppermute | solution.py:20
  7.8 6.5 %collective-permute-start = (bf16[512,128]{1,0:T(8,128)(2,1)S(1)}, bf16[512,128]{1,0:T(8,128)(2,1)S(1)}, u32[]{:S(2)}, u32[]{:S(2)}) collective-permute-start(bf16[512,128]{1,0:T(8,128)(2,1)S(1)} %get-tuple-element.25), channel_id=1, source_target_pairs={{0,8},{8,0},{1,9},{9,1},{2,10},{10,2},{3,11},{11,3},{4,12},{12,4},... | collective-permute-start | bytes 393224 | tf_op jit(solution)/shard_map/ppermute | solution.py:24
  16.1 9.8 %collective-permute-start.6 = (bf16[1536,128]{1,0:T(8,128)(2,1)S(1)}, bf16[1536,128]{1,0:T(8,128)(2,1)S(1)}, u32[]{:S(2)}, u32[]{:S(2)}) collective-permute-start(bf16[1536,128]{1,0:T(8,128)(2,1)S(1)} %get-tuple-element.26), channel_id=1, source_target_pairs={{0,7},{1,0},{2,1},{3,2},{4,3},{5,4},{6,5},{7,6},{8,15},{9,8},{10,9... | collective-permute-start | bytes 1179656 | tf_op jit(solution)/shard_map/ppermute | solution.py:20
  17.6 10.7 %collective-permute-start.5 = (bf16[1536,128]{1,0:T(8,128)(2,1)S(1)}, bf16[1536,128]{1,0:T(8,128)(2,1)S(1)}, u32[]{:S(2)}, u32[]{:S(2)}) collective-permute-start(bf16[1536,128]{1,0:T(8,128)(2,1)S(1)} %get-tuple-element.27), channel_id=1, source_target_pairs={{0,1},{1,2},{2,3},{3,4},{4,5},{5,6},{6,7},{7,0},{8,9},{9,10},{10,1... | collective-permute-start | bytes 1179656 | tf_op jit(solution)/shard_map/ppermute | solution.py:20
  25.9 9.2 %collective-permute-start.9 = (bf16[1536,128]{1,0:T(8,128)(2,1)S(1)}, bf16[1536,128]{1,0:T(8,128)(2,1)S(1)}, u32[]{:S(2)}, u32[]{:S(2)}) collective-permute-start(bf16[1536,128]{1,0:T(8,128)(2,1)S(1)} %collective-permute-done.6.refs_11_), channel_id=1, source_target_pairs={{0,7},{1,0},{2,1},{3,2},{4,3},{5,4},{6,5},{7,6},{8,15},{9,8},{10,9... | collective-permute-start | bytes 1179656 | tf_op jit(solution)/shard_map/ppermute | solution.py:20
  28.3 9.9 %collective-permute-start.8 = (bf16[1536,128]{1,0:T(8,128)(2,1)S(1)}, bf16[1536,128]{1,0:T(8,128)(2,1)S(1)}, u32[]{:S(2)}, u32[]{:S(2)}) collective-permute-start(bf16[1536,128]{1,0:T(8,128)(2,1)S(1)} %collective-permute-done.5.refs_10_), channel_id=1, source_target_pairs={{0,1},{1,2},{2,3},{3,4},{4,5},{5,6},{6,7},{7,0},{8,9},{9,10},{10,1... | collective-permute-start | bytes 1179656 | tf_op jit(solution)/shard_map/ppermute | solution.py:20
  35.1 9.0 %collective-permute-start.12 = (bf16[1024,128]{1,0:T(8,128)(2,1)S(1)}, bf16[1024,128]{1,0:T(8,128)(2,1)S(1)}, u32[]{:S(2)}, u32[]{:S(2)}) collective-permute-start(bf16[1024,128]{1,0:T(8,128)(2,1)S(1)} %slice.138), channel_id=1, source_target_pairs={{0,7},{1,0},{2,1},{3,2},{4,3},{5,4},{6,5},{7,6},{8,15},{9,8},{10,9... | collective-permute-start | bytes 786440 | tf_op jit(solution)/shard_map/ppermute | solution.py:20
  38.2 7.7 %collective-permute-start.11 = (bf16[1024,128]{1,0:T(8,128)(2,1)S(1)}, bf16[1024,128]{1,0:T(8,128)(2,1)S(1)}, u32[]{:S(2)}, u32[]{:S(2)}) collective-permute-start(bf16[1024,128]{1,0:T(8,128)(2,1)S(1)} %pad_maximum_fusion.6), channel_id=1, source_target_pairs={{0,1},{1,2},{2,3},{3,4},{4,5},{5,6},{6,7},{7,0},{8,9},{9,10},{10,1... | collective-permute-start | bytes 786440 | tf_op jit(solution)/shard_map/ppermute | solution.py:20
  39.0 26.0 %collective-permute-start.4 = (bf16[1024,128]{1,0:T(8,128)(2,1)}, bf16[1024,128]{1,0:T(8,128)(2,1)S(1)}, u32[]{:S(2)}, u32[]{:S(2)}) collective-permute-start(bf16[1024,128]{1,0:T(8,128)(2,1)} %pad_maximum_fusion.3), channel_id=1, source_target_pairs={{0,8},{8,0},{1,9},{9,1},{2,10},{10,2},{3,11},{11,3},{4,12},{12,4},... | collective-permute-start | bytes 786440 | tf_op jit(solution)/shard_map/ppermute | solution.py:24
  39.8 25.3 %collective-permute-start.7 = (bf16[1024,128]{1,0:T(8,128)(2,1)}, bf16[1024,128]{1,0:T(8,128)(2,1)}, u32[]{:S(2)}, u32[]{:S(2)}) collective-permute-start(bf16[1024,128]{1,0:T(8,128)(2,1)} %pad_maximum_fusion.4), channel_id=1, source_target_pairs={{0,8},{8,0},{1,9},{9,1},{2,10},{10,2},{3,11},{11,3},{4,12},{12,4},... | collective-permute-start | bytes 786440 | tf_op jit(solution)/shard_map/ppermute | solution.py:24
  44.1 21.0 %collective-permute-start.10 = (bf16[1024,128]{1,0:T(8,128)(2,1)}, bf16[1024,128]{1,0:T(8,128)(2,1)}, u32[]{:S(2)}, u32[]{:S(2)}) collective-permute-start(bf16[1024,128]{1,0:T(8,128)(2,1)} %pad_maximum_fusion.5), channel_id=1, source_target_pairs={{0,8},{8,0},{1,9},{9,1},{2,10},{10,2},{3,11},{11,3},{4,12},{12,4},... | collective-permute-start | bytes 786440 | tf_op jit(solution)/shard_map/ppermute | solution.py:24
  46.6 18.4 %collective-permute-start.13 = (bf16[1024,128]{1,0:T(8,128)(2,1)}, bf16[1024,128]{1,0:T(8,128)(2,1)}, u32[]{:S(2)}, u32[]{:S(2)}) collective-permute-start(bf16[1024,128]{1,0:T(8,128)(2,1)} %pad_maximum_fusion.7), channel_id=1, source_target_pairs={{0,8},{8,0},{1,9},{9,1},{2,10},{10,2},{3,11},{11,3},{4,12},{12,4},... | collective-permute-start | bytes 786440 | tf_op jit(solution)/shard_map/ppermute | solution.py:24
  48.4 16.7 %collective-permute-start.1 = (bf16[512,128]{1,0:T(8,128)(2,1)}, bf16[512,128]{1,0:T(8,128)(2,1)S(1)}, u32[]{:S(2)}, u32[]{:S(2)}) collective-permute-start(bf16[512,128]{1,0:T(8,128)(2,1)} %get-tuple-element.24), channel_id=1, source_target_pairs={{0,8},{8,0},{1,9},{9,1},{2,10},{10,2},{3,11},{11,3},{4,12},{12,4},... | collective-permute-start | bytes 393224 | tf_op jit(solution)/shard_map/ppermute | solution.py:24
  65.1 40.5 %copy-start.1 = (f32[1,1024]{1,0:T(1,128)S(1)}, f32[1,1024]{1,0:T(1,128)}, u32[]{:S(2)}) copy-start(f32[1,1024]{1,0:T(1,128)} %param.11) | copy-start | bytes 12292
  65.1 40.7 %copy-start.2 = (f32[128]{0:T(128)S(1)}, f32[128]{0:T(128)}, u32[]{:S(2)}) copy-start(f32[128]{0:T(128)} %param.17) | copy-start | bytes 1540
  68.9 2.7 %collective-permute-start.19 = (bf16[4,2,4,128,128]{4,3,2,1,0:T(8,128)(2,1)S(1)}, bf16[4,2,4,128,128]{4,3,2,1,0:T(8,128)(2,1)S(1)}, u32[]{:S(2)}, u32[]{:S(2)}) collective-permute-start(bf16[4,2,4,128,128]{4,3,2,1,0:T(8,128)(2,1)S(1)} %get-tuple-element.12), channel_id=1, source_target_pairs={{0,16},{16,0},{1,17},{17,1},{2,18},{18,2},{3,19},{19,3},{4,20},{20... | collective-permute-start | bytes 3145736 | tf_op jit(solution)/shard_map/ppermute | solution.py:24
  69.0 12.6 %collective-permute-start.14 = (bf16[2,4,4,128,128]{4,3,2,1,0:T(8,128)(2,1)S(1)}, bf16[2,4,4,128,128]{4,3,2,1,0:T(8,128)(2,1)S(1)}, u32[]{:S(2)}, u32[]{:S(2)}) collective-permute-start(bf16[2,4,4,128,128]{4,3,2,1,0:T(8,128)(2,1)S(1)} %get-tuple-element.10), channel_id=1, source_target_pairs={{0,16},{16,0},{1,17},{17,1},{2,18},{18,2},{3,19},{19,3},{4,20},{20... | collective-permute-start | bytes 3145736 | tf_op jit(solution)/shard_map/ppermute | solution.py:24
  71.8 13.7 %collective-permute-start.20 = (bf16[2,4,128,128]{3,2,1,0:T(8,128)(2,1)S(1)}, bf16[2,4,128,128]{3,2,1,0:T(8,128)(2,1)S(1)}, u32[]{:S(2)}, u32[]{:S(2)}) collective-permute-start(bf16[2,4,128,128]{3,2,1,0:T(8,128)(2,1)S(1)} %get-tuple-element.15), channel_id=1, source_target_pairs={{0,32},{32,64},{64,96},{96,0},{1,33},{33,65},{65,97},{97,1},{2,34}... | collective-permute-start | bytes 786440 | tf_op jit(solution)/shard_map/ppermute | solution.py:20
  78.8 11.5 %collective-permute-start.22 = (bf16[2,4,128,128]{3,2,1,0:T(8,128)(2,1)S(1)}, bf16[2,4,128,128]{3,2,1,0:T(8,128)(2,1)S(1)}, u32[]{:S(2)}, u32[]{:S(2)}) collective-permute-start(bf16[2,4,128,128]{3,2,1,0:T(8,128)(2,1)S(1)} %get-tuple-element.16), channel_id=1, source_target_pairs={{0,64},{32,96},{64,0},{96,32},{1,65},{33,97},{65,1},{97,33},{2,66}... | collective-permute-start | bytes 786440 | tf_op jit(solution)/shard_map/ppermute | solution.py:20
  78.8 12.4 %collective-permute-start.21 = (bf16[2,4,128,128]{3,2,1,0:T(8,128)(2,1)S(1)}, bf16[2,4,128,128]{3,2,1,0:T(8,128)(2,1)S(1)}, u32[]{:S(2)}, u32[]{:S(2)}) collective-permute-start(bf16[2,4,128,128]{3,2,1,0:T(8,128)(2,1)S(1)} %get-tuple-element.17), channel_id=1, source_target_pairs={{0,96},{32,0},{64,32},{96,64},{1,97},{33,1},{65,33},{97,65},{2,98}... | collective-permute-start | bytes 786440 | tf_op jit(solution)/shard_map/ppermute | solution.py:20
  81.8 14.9 %collective-permute-start.15 = (bf16[4,4,128,128]{3,2,1,0:T(8,128)(2,1)S(1)}, bf16[4,4,128,128]{3,2,1,0:T(8,128)(2,1)S(1)}, u32[]{:S(2)}, u32[]{:S(2)}) collective-permute-start(bf16[4,4,128,128]{3,2,1,0:T(8,128)(2,1)S(1)} %fusion.3), channel_id=1, source_target_pairs={{0,128},{128,0},{1,129},{129,1},{2,130},{130,2},{3,131},{131,3},{4... | collective-permute-start | bytes 1572872 | tf_op jit(solution)/shard_map/ppermute | solution.py:24
  91.4 8.8 %collective-permute-start.23 = (bf16[4,128,128]{2,1,0:T(8,128)(2,1)S(1)}, bf16[4,128,128]{2,1,0:T(8,128)(2,1)S(1)}, u32[]{:S(2)}, u32[]{:S(2)}) collective-permute-start(bf16[4,128,128]{2,1,0:T(8,128)(2,1)S(1)} %fusion.14), channel_id=1, source_target_pairs={{0,128},{128,0},{1,129},{129,1},{2,130},{130,2},{3,131},{131,3},{4... | collective-permute-start | bytes 393224 | tf_op jit(solution)/shard_map/ppermute | solution.py:24
  96.9 7.7 %collective-permute-start.16 = (bf16[4,128,128]{2,1,0:T(8,128)(2,1)S(1)}, bf16[4,128,128]{2,1,0:T(8,128)(2,1)S(1)}, u32[]{:S(2)}, u32[]{:S(2)}) collective-permute-start(bf16[4,128,128]{2,1,0:T(8,128)(2,1)S(1)} %get-tuple-element.18), channel_id=1, source_target_pairs={{0,32},{32,64},{64,96},{96,0},{1,33},{33,65},{65,97},{97,1},{2,34}... | collective-permute-start | bytes 393224 | tf_op jit(solution)/shard_map/ppermute | solution.py:20
  97.0 7.6 %collective-permute-start.18 = (bf16[4,128,128]{2,1,0:T(8,128)(2,1)S(1)}, bf16[4,128,128]{2,1,0:T(8,128)(2,1)S(1)}, u32[]{:S(2)}, u32[]{:S(2)}) collective-permute-start(bf16[4,128,128]{2,1,0:T(8,128)(2,1)S(1)} %get-tuple-element.19), channel_id=1, source_target_pairs={{0,64},{32,96},{64,0},{96,32},{1,65},{33,97},{65,1},{97,33},{2,66}... | collective-permute-start | bytes 393224 | tf_op jit(solution)/shard_map/ppermute | solution.py:20
  98.1 7.4 %collective-permute-start.17 = (bf16[4,128,128]{2,1,0:T(8,128)(2,1)S(1)}, bf16[4,128,128]{2,1,0:T(8,128)(2,1)S(1)}, u32[]{:S(2)}, u32[]{:S(2)}) collective-permute-start(bf16[4,128,128]{2,1,0:T(8,128)(2,1)S(1)} %get-tuple-element.20), channel_id=1, source_target_pairs={{0,96},{32,0},{64,32},{96,64},{1,97},{33,1},{65,33},{97,65},{2,98}... | collective-permute-start | bytes 393224 | tf_op jit(solution)/shard_map/ppermute | solution.py:20

commit v3 on v0

v3 whole, which is shorter than its diff:
```python
import jax
import jax.numpy as jnp
from jax import lax
from jax.experimental import pallas as pl
from jax.experimental.pallas import tpu as pltpu
from jax.sharding import Mesh
from jax.sharding import PartitionSpec as P


ROW = ("xl", "y", "core")
COL = ("xh", "z")
BF16 = jnp.bfloat16
F32 = jnp.float32


def swapped(value, axis, partner):
    n = lax.axis_size(axis)
    return lax.ppermute(value, axis, [(i, partner(i) % n) for i in range(n)])


def other(i):
    return i ^ 1


def other_side(i):
    return i + (i & 1) * 2 - 1


def gathered(own):
    half = own.shape[0] // 2
    found = {(0, 0, 0): (own, 0), (0, 0, 1): (own, half)}
    across = swapped(own, "xh", other)
    near = swapped(own, "z", other)
    back = swapped(own, "z", other_side)
    other_top = across[:half]
    found[1, 0, 0] = (across, 0)
    found[1, 0, 1] = (across, half)
    for step in (1, 2, 3):
        for sign, value in ((1, near), (-1, back)):
            found[0, sign * step, 0] = (value, 0)
            found[0, sign * step, 1] = (value, half)
            if step > 1:
                found[1, sign * (step - 1), 0] = (value, 2 * half)
        if step == 1:
            from_near = jnp.concatenate([near, other_top])
            from_back = jnp.concatenate([back, other_top])
        elif step == 2:
            from_near, from_back = near, back
        else:
            from_near = near[half:]
            from_back = jnp.concatenate([back[:half], back[2 * half :]])
        lows = jnp.concatenate([near[half : 2 * half], back[half : 2 * half]])
        near = swapped(from_back, "z", other)
        back = swapped(from_near, "z", other_side)
        lows = swapped(lows, "xh", other)
        found[1, step, 1] = (lows, 0)
        found[1, -step, 1] = (lows, half)
    found[0, 4, 0] = (near, 0)
    found[0, 4, 1] = (back, 0)
    found[1, 3, 0] = (near, half)
    found[1, -3, 0] = (back, half)
    last = swapped(jnp.concatenate([near[:half], back[:half]]), "xh", other)
    found[1, 4, 0] = (last, 0)
    found[1, 4, 1] = (last, half)
    return found


PHASES = 3
BLOCK = 16
STEP = 4
CAP = 320 + STEP
SHARES = (688, 336)
HALVINGS = ((("xl", 1, 3), (1, 3, "xl")), ((3, "xl", 1), (3, "xl", 1)))


def phase_of(key):
    dx, dz, half = key
    far = abs(dz)
    if not dx:
        return (0, 0, 0, 1, 1)[far]
    return ((0, 0, 1, 1, 2), (0, 0, 1, 2, 2))[half][far]


def place():
    z = lax.axis_index("z")
    return lax.axis_index("xh"), z, 1 - 2 * (z & 1)


def prepare(keys, count_ref, row_ref, col_ref, tiles_hbm, acc, codes, tiles, tile_sem):
    fetch = pltpu.make_async_copy(tiles_hbm.at[0, 0], tiles, tile_sem)
    fetch.start()
    zeros = jnp.zeros((128, acc.shape[1]), acc.dtype)

    @pl.loop(0, acc.shape[0] // 128)
    def _(d):
        acc[pl.ds(pl.multiple_of(d * 128, 128), 128)] = zeros

    count = count_ref[0, 0]
    xh, z, sign = place()
    flip = (sign - 1) >> 1
    start = z ^ flip
    tables = [0, 0]
    for dx, dz, half in keys:
        tables[dx] |= phase_of((dx, dz, half)) << ((dz & 7) * 4 + half * 2)
    tables = [jnp.int32(m - (1 << 32) if m >> 31 else m) for m in tables]
    near_table = jnp.where(xh == 0, tables[0], tables[1])
    far_table = jnp.where(xh == 0, tables[1], tables[0])

    def list_slots(k, counts):
        for u in range(STEP):
            t = k * STEP + u
            col = col_ref[0, 0, t]
            shift = ((((col >> 3) ^ flip) - start) & 7) * 4 + ((col >> 1) & 2)
            phase = (jnp.where(col < 64, near_table, far_table) >> shift) & 3
            field = phase * 10
            codes[phase * CAP + ((counts >> field) & 1023)] = (
                t | (row_ref[0, 0, t] << 9) | (col << 17)
            )
            counts = counts + ((((t - count) >> 31) & 1) << field)
        return counts

    counts = lax.fori_loop(0, (count + STEP - 1) // STEP, list_slots, jnp.int32(0))
    for p in range(PHASES):
        n = (counts >> (10 * p)) & 1023
        codes[PHASES * CAP + p] = n
        for i in range(STEP):
            codes[p * CAP + n + i] = jnp.int32((acc.shape[0] // 128 - 1) << 9)
    fetch.wait()


def prepared(keys, count, row_ids, col_ids, tiles, dests):
    side, width = tiles.shape[3:]

    def kernel(*refs):
        prepare(keys, *refs)

    smem, vmem = (pl.BlockSpec(memory_space=m) for m in (pltpu.SMEM, pltpu.VMEM))
    return pl.pallas_call(
        kernel,
        out_shape=(
            jax.ShapeDtypeStruct(((dests + 1) * side, width), F32),
            jax.ShapeDtypeStruct((PHASES * CAP + PHASES,), jnp.int32),
            jax.ShapeDtypeStruct(tiles.shape[2:], tiles.dtype),
        ),
        in_specs=[smem] * 3 + [pl.BlockSpec(memory_space=pltpu.HBM)],
        out_specs=(vmem, smem, vmem),
        scratch_shapes=[pltpu.SemaphoreType.DMA],
        compiler_params=pltpu.CompilerParams(vmem_limit_bytes=34 * 2**20),
        name="prepare",
    )(count, row_ids, col_ids, tiles)


def add_products(phase, places, codes, tiles, parts, feat, acc):
    xh, z, sign = place()
    for (dx, dz, half), (part, row) in places.items():
        block = ((xh ^ dx) * 8 + ((z + sign * dz) & 7)) * 8 + half * 4
        for i in range(4):
            feat[block + i] = parts[part][row + i * 128 : row + (i + 1) * 128]

    def run(first, size):
        for start in range(0, size, STEP):
            entries = [codes[phase * CAP + first + start + u] for u in range(STEP)]
            products = [
                jnp.dot(tiles[e & 511], feat[e >> 17], preferred_element_type=F32)
                for e in entries
            ]
            for e, product in zip(entries, products):
                acc[pl.ds(pl.multiple_of(((e >> 9) & 255) * 128, 128), 128)] += product

    count = codes[PHASES * CAP + phase]
    whole = count // BLOCK

    @pl.loop(0, whole)
    def _(k):
        run(k * BLOCK, BLOCK)

    @pl.loop(0, (count - whole * BLOCK + STEP - 1) // STEP)
    def _(k):
        run(whole * BLOCK + k * STEP, STEP)


def parts_of(found, phase):
    mine = {key: at for key, at in found.items() if phase_of(key) == phase}
    parts = list({id(value): value for value, _ in mine.values()}.values())
    index = {id(value): i for i, value in enumerate(parts)}
    return parts, {key: (index[id(value)], row) for key, (value, row) in mine.items()}


def phase_sums(phase, codes, tiles, acc, found):
    parts, places = parts_of(found, phase)
    n = len(parts)

    def kernel(codes_ref, tiles_ref, acc_in, *refs):
        add_products(phase, places, codes_ref, tiles_ref, refs[:n], refs[n + 1], refs[n])

    smem, vmem = (pl.BlockSpec(memory_space=m) for m in (pltpu.SMEM, pltpu.VMEM))
    return pl.pallas_call(
        kernel,
        out_shape=jax.ShapeDtypeStruct(acc.shape, acc.dtype),
        in_specs=[smem, vmem, vmem] + [vmem] * n,
        out_specs=vmem,
        scratch_shapes=[pltpu.VMEM((128, *tiles.shape[1:]), BF16)],
        input_output_aliases={2: 0},
        compiler_params=pltpu.CompilerParams(vmem_limit_bytes=16 * 2**20),
    )(codes, tiles, acc, *parts)


def write_part(acc, part, keep, send):
    xl, y, core = (lax.axis_index(a) for a in ROW)

    @pl.loop(0, 8)
    def _(at):
        bits = (at >> 2, (at >> 1) & 1, at & 1)
        for mine, out in ((0, keep), (1, send)):
            dest_core = core ^ mine
            turns = [dict(zip(kinds, bits)) for kinds in HALVINGS[part]]
            turn = {k: jnp.where(dest_core == 0, turns[0][k], turns[1][k]) for k in turns[0]}
            device = ((xl ^ turn["xl"]) * 4 + (y ^ turn[1] ^ (3 * turn[3]))) * 2 + dest_core
            row = device * sum(SHARES) + sum(SHARES[:part])
            rows = acc[pl.ds(pl.multiple_of(row, 16), SHARES[part])]
            out[at] = rows.astype(BF16)


def last_sums(codes, tiles, acc, found):
    phase = PHASES - 1
    parts, places = parts_of(found, phase)
    n = len(parts)
    side, width = tiles.shape[1:]

    def kernel(codes_ref, tiles_ref, acc_in, *refs):
        sums, keep, send, feat = refs[n:]
        add_products(phase, places, codes_ref, tiles_ref, refs[:n], feat, sums)
        write_part(sums, 0, keep, send)

    def rest(acc_ref, keep, send):
        write_part(acc_ref, 1, keep, send)

    smem, vmem = (pl.BlockSpec(memory_space=m) for m in (pltpu.SMEM, pltpu.VMEM))
    out_a = jax.ShapeDtypeStruct((8, SHARES[0], width), BF16)
    out_b = jax.ShapeDtypeStruct((8, SHARES[1], width), BF16)
    params = pltpu.CompilerParams(vmem_limit_bytes=16 * 2**20)
    acc, keep_a, send_a = pl.pallas_call(
        kernel,
        out_shape=(jax.ShapeDtypeStruct(acc.shape, acc.dtype), out_a, out_a),
        in_specs=[smem, vmem, vmem] + [vmem] * n,
        out_specs=(vmem, vmem, vmem),
        scratch_shapes=[pltpu.VMEM((128, side, width), BF16)],
        input_output_aliases={2: 0},
        compiler_params=params,
    )(codes, tiles, acc, *parts)
    keep_b, send_b = pl.pallas_call(
        rest,
        out_shape=(out_b, out_b),
        in_specs=[vmem],
        out_specs=(vmem, vmem),
        compiler_params=params,
        name="rest",
    )(acc)
    return keep_a, send_a, keep_b, send_b


def added(*values):
    total = values[0].astype(F32)
    for value in values[1:]:
        total = total + value.astype(F32)
    return total


def halved(value, part, step):
    def partner(i):
        xl, y, core = i >> 3, (i >> 1) & 3, i & 1
        kind = HALVINGS[part][core][step]
        return (((xl ^ 1) * 4 + y) if kind == "xl" else (xl * 4 + (y ^ kind))) * 2 + core

    return lax.ppermute(value, ROW, [(i, partner(i)) for i in range(16)])


def scattered(keep_a, send_a, keep_b, send_b):
    held = [[keep_a, swapped(send_a, "core", other)], [keep_b, swapped(send_b, "core", other)]]
    for step in range(3):
        size = 4 >> step
        came = [
            halved(added(*(v[size:] for v in values)).astype(BF16), part, step)
            for part, values in enumerate(held)
        ]
        held = [[v[:size] for v in values] + [new] for values, new in zip(held, came)]
    return jnp.concatenate([added(*values)[0] for values in held])


def shards(
    node_features, src_norm, dst_norm, tiles, row_block, col_block, tile_count, weight, bias
):
    scaled = (src_norm[:, None] * node_features.astype(F32)).astype(BF16)
    dests = dst_norm.shape[1] * 16 // tiles.shape[-1]
    found = gathered(scaled)
    acc, codes, held = prepared(
        list(found), tile_count, row_block, col_block, tiles, dests
    )
    for phase in range(PHASES - 1):
        acc = phase_sums(phase, codes, held, acc, found)
    sums = last_sums(codes, held, acc, found)
    aggregate = scattered(*sums)
    hidden = (dst_norm[0][:, None] * aggregate).astype(BF16)
    mixed = jnp.dot(hidden, weight, preferred_element_type=F32) + bias
    return jnp.maximum(mixed, 0.0).astype(BF16)[None]


def solution(mesh):
    torus = Mesh(mesh.devices.reshape(2, 4, 2, 2, 8), ROW + COL)
    in_specs = (
        P(ROW + COL, None),
        P(ROW + COL),
        P(COL, ROW),
        P(ROW, COL, None, None, None),
        P(ROW, COL, None),
        P(ROW, COL, None),
        P(ROW, COL),
        P(),
        P(),
    )
    out_specs = P(COL, ROW, None)

    return jax.shard_map(
        shards, mesh=torus, in_specs=in_specs, out_specs=out_specs, check_vma=False
    )
```

time: 222 us -> 99.3 us (0.45)
  waiting for transfers between devices: 123 us -> 48.6 us
  local copies, waits for them, and re-layouts: 39.4 us -> 0.15 us
  starting transfers between devices: 0.04 us -> 36.1 us
  matrix products: 30.5 us -> 1.03 us
  between operations: 14.1 us -> 0.94 us
  blocking collectives: 10.3 us -> 0 us
  Pallas kernels: 0 us -> 9.14 us
    reduce_scatter x1 -> x0, waiting for transfers between devices: 68.4 us -> none  [shards(): lax.psum_scatter(partial_sum.astype(jnp.bfloat16), 'row', scatter_dimensi...]
    all_gather x1 -> x0, waiting for transfers between devices: 55 us -> none  [gather_in_order(): pieces = lax.all_gather(pieces, axes[k], axis=0, tiled=True)]
    ppermute x0 -> x21, waiting for transfers between devices: none -> 48.6 us  [the longest x15 29.6 us: swapped(): return lax.ppermute(value, axis, [(i, partner(i) % n) for i in range(n)])]
    ppermute x0 -> x21, starting transfers between devices: none -> 36.1 us  [the longest x15 25 us: swapped(): return lax.ppermute(value, axis, [(i, partner(i) % n) for i in range(n)])]
    dot_general x3 -> x1, matrix products: 30.5 us -> 1.03 us  [shards(): mixed = jnp.dot(hidden, weight, preferred_element_type=F32) + bias]
    dot_general x1 -> x0, local copies, waits for them, and re-layouts: 14.4 us -> none  [shards(): jnp.einsum('tij,tjf->tif', tile_set, picked, preferred_element_type=jnp.f...]
    gather x1 -> x0, local copies, waits for them, and re-layouts: 12.9 us -> none  [shards(): picked = jnp.take(blocks, col_ids, axis=0)]
    all_gather x1 -> x0, blocking collectives: 10.3 us -> none  [gather_in_order(): pieces = lax.all_gather(pieces, axes[k], axis=0, tiled=True)]
  transfers between devices with their start and end apart: 2 -> 21, of which waited for: 2 -> 13; matrix products, arithmetic and copies ran while one was open for 1% -> 1% of each run, Pallas kernels for 0% -> 8%
where the time goes in v3:
time: 99.3 us; the launch traced here: 98.1 us
  waiting for transfers between devices  48.6 us (49%)
  starting transfers between devices  36.1 us (36%)
  Pallas kernels  9.14 us (9%)
  other arithmetic  2.11 us (2%)
  matrix products  1.03 us (1%)
    ppermute x15, waiting for transfers between devices, swapped(): return lax.ppermute(value, axis, [(i, partner(i) % n) for i in range(n)])  29.6 us
    ppermute x15, starting transfers between devices, swapped(): return lax.ppermute(value, axis, [(i, partner(i) % n) for i in range(n)])  25 us
    ppermute x6, waiting for transfers between devices, halved(): return lax.ppermute(value, ROW, [(i, partner(i)) for i in range(16)])  19 us
    ppermute x6, starting transfers between devices, halved(): return lax.ppermute(value, ROW, [(i, partner(i)) for i in range(16)])  11.1 us
    pallas_call x1, Pallas kernels, prepared(): pl.pallas_call(kernel, out_shape=(jax.ShapeDtypeStruct(((dests + 1) * sid...  5.22 us
    pallas_call x2, Pallas kernels, phase_sums(): pl.pallas_call(kernel, out_shape=jax.ShapeDtypeStruct(acc.shape, acc.dtyp...  2.51 us
  transfers between devices with their start and end apart: 21, of which 13 were waited for; matrix products, arithmetic and copies ran while one was open for 1% of the time, Pallas kernels for 8%

profile of v3, /device:TPU:4, one launch (start us, length us, event | category | flops | bytes accessed | tf_op | source)
XLA Modules:
  0.0 98.1 jit_solution(11364750120834585935)
XLA Ops:
  0.0 0.0 copy-start
  0.0 1.2 %multiply_convert_fusion.refs_0_ = bf16[1024,128]{1,0:T(8,128)(2,1)S(1)} fusion(bf16[1024,128]{1,0:T(8,128)(2,1)} %param.9, f32[1024]{0:T(1024)} %param.10), kind=kLoop, calls=%fused_computation.9 | loop fusion | flops 393216 | bytes 528384 | tf_op jit(solution)/shard_map/convert_element_type | solution.py:293
  1.2 2.3 %collective-permute-start = (bf16[1024,128]{1,0:T(8,128)(2,1)S(1)}, bf16[1024,128]{1,0:T(8,128)(2,1)S(1)}, u32[]{:S(2)}, u32[]{:S(2)}) collective-permute-start(bf16[1024,128]{1,0:T(8,128)(2,1)S(1)} %multiply_convert_fusion.refs_0_), channel_id=1, source_target_pairs={{0,8},{8,0},{1,9},{9,1},{2,10},{10,2},{3,11},{11,3},{4,12},{12,4},... | collective-permute-start | bytes 786440 | tf_op jit(solution)/shard_map/ppermute | solution.py:18
  3.5 0.2 collective-permute-start.1
  3.7 4.9 %collective-permute-start.2 = (bf16[1024,128]{1,0:T(8,128)(2,1)S(1)}, bf16[1024,128]{1,0:T(8,128)(2,1)S(1)}, u32[]{:S(2)}, u32[]{:S(2)}) collective-permute-start(bf16[1024,128]{1,0:T(8,128)(2,1)S(1)} %multiply_convert_fusion.refs_0_), channel_id=1, source_target_pairs={{0,7},{1,2},{2,1},{3,4},{4,3},{5,6},{6,5},{7,0},{8,15},{9,10},{10,... | collective-permute-start | bytes 786440 | tf_op jit(solution)/shard_map/ppermute | solution.py:18
  8.6 2.2 %collective-permute-done.refs_1_ = bf16[1024,128]{1,0:T(8,128)(2,1)S(1)} collective-permute-done((bf16[1024,128]{1,0:T(8,128)(2,1)S(1)}, bf16[1024,128]{1,0:T(8,128)(2,1)S(1)}, u32[]{:S(2)}, u32[]{:S(2)}) %collective-permute-start) | collective-permute-done | bytes 262176 | tf_op jit(solution)/shard_map/ppermute | solution.py:18
  10.8 0.0 collective-permute-done.1.refs_2_
  10.8 3.5 %collective-permute-done.2.refs_3_ = bf16[1024,128]{1,0:T(8,128)(2,1)S(1)} collective-permute-done((bf16[1024,128]{1,0:T(8,128)(2,1)S(1)}, bf16[1024,128]{1,0:T(8,128)(2,1)S(1)}, u32[]{:S(2)}, u32[]{:S(2)}) %collective-permute-start.2) | collective-permute-done | bytes 262176 | tf_op jit(solution)/shard_map/ppermute | solution.py:18
  14.4 0.1 pad_maximum_fusion
  14.4 0.1 collective-permute-start.4
  14.5 3.3 %collective-permute-start.5 = (bf16[1536,128]{1,0:T(8,128)(2,1)S(1)}, bf16[1536,128]{1,0:T(8,128)(2,1)S(1)}, u32[]{:S(2)}, u32[]{:S(2)}) collective-permute-start(bf16[1536,128]{1,0:T(8,128)(2,1)S(1)} %get-tuple-element.24), channel_id=1, source_target_pairs={{0,7},{1,2},{2,1},{3,4},{4,3},{5,6},{6,5},{7,0},{8,15},{9,10},{10,... | collective-permute-start | bytes 1179656 | tf_op jit(solution)/shard_map/ppermute | solution.py:18
  17.9 6.4 %collective-permute-done.4.refs_5_ = bf16[1536,128]{1,0:T(8,128)(2,1)S(1)} collective-permute-done((bf16[1536,128]{1,0:T(8,128)(2,1)S(1)}, bf16[1536,128]{1,0:T(8,128)(2,1)S(1)}, u32[]{:S(2)}, u32[]{:S(2)}) %collective-permute-start.4) | collective-permute-done | bytes 393248 | tf_op jit(solution)/shard_map/ppermute | solution.py:18
  24.2 2.7 %collective-permute-start.8 = (bf16[1536,128]{1,0:T(8,128)(2,1)S(1)}, bf16[1536,128]{1,0:T(8,128)(2,1)S(1)}, u32[]{:S(2)}, u32[]{:S(2)}) collective-permute-start(bf16[1536,128]{1,0:T(8,128)(2,1)S(1)} %collective-permute-done.4.refs_5_), channel_id=1, source_target_pairs={{0,7},{1,2},{2,1},{3,4},{4,3},{5,6},{6,5},{7,0},{8,15},{9,10},{10,... | collective-permute-start | bytes 1179656 | tf_op jit(solution)/shard_map/ppermute | solution.py:18
  26.9 0.0 collective-permute-done.5.refs_6_
  26.9 0.0 collective-permute-start.7
  26.9 7.4 %collective-permute-done.8.refs_2_ = bf16[1536,128]{1,0:T(8,128)(2,1)S(1)} collective-permute-done((bf16[1536,128]{1,0:T(8,128)(2,1)S(1)}, bf16[1536,128]{1,0:T(8,128)(2,1)S(1)}, u32[]{:S(2)}, u32[]{:S(2)}) %collective-permute-start.8) | collective-permute-done | bytes 393248 | tf_op jit(solution)/shard_map/ppermute | solution.py:18
  34.4 0.2 collective-permute-start.9
  34.5 1.8 %collective-permute-done.7.refs_1_ = bf16[1536,128]{1,0:T(8,128)(2,1)S(1)} collective-permute-done((bf16[1536,128]{1,0:T(8,128)(2,1)S(1)}, bf16[1536,128]{1,0:T(8,128)(2,1)S(1)}, u32[]{:S(2)}, u32[]{:S(2)}) %collective-permute-start.7) | collective-permute-done | bytes 393248 | tf_op jit(solution)/shard_map/ppermute | solution.py:18
  36.4 1.8 %collective-permute-start.10 = (bf16[1024,128]{1,0:T(8,128)(2,1)S(1)}, bf16[1024,128]{1,0:T(8,128)(2,1)S(1)}, u32[]{:S(2)}, u32[]{:S(2)}) collective-permute-start(bf16[1024,128]{1,0:T(8,128)(2,1)S(1)} %slice.189), channel_id=1, source_target_pairs={{0,7},{1,2},{2,1},{3,4},{4,3},{5,6},{6,5},{7,0},{8,15},{9,10},{10,... | collective-permute-start | bytes 786440 | tf_op jit(solution)/shard_map/ppermute | solution.py:18
  38.3 0.0 copy-start.1
  38.3 0.0 copy-start.2
  38.3 2.4 %collective-permute-start.3 = (bf16[1024,128]{1,0:T(8,128)(2,1)S(1)}, bf16[1024,128]{1,0:T(8,128)(2,1)S(1)}, u32[]{:S(2)}, u32[]{:S(2)}) collective-permute-start(bf16[1024,128]{1,0:T(8,128)(2,1)S(1)} %pad_maximum_fusion.2), channel_id=1, source_target_pairs={{0,8},{8,0},{1,9},{9,1},{2,10},{10,2},{3,11},{11,3},{4,12},{12,4},... | collective-permute-start | bytes 786440 | tf_op jit(solution)/shard_map/ppermute | solution.py:18
  40.8 1.3 %collective-permute-start.6 = (bf16[1024,128]{1,0:T(8,128)(2,1)S(1)}, bf16[1024,128]{1,0:T(8,128)(2,1)S(1)}, u32[]{:S(2)}, u32[]{:S(2)}) collective-permute-start(bf16[1024,128]{1,0:T(8,128)(2,1)S(1)} %pad_maximum_fusion.3), channel_id=1, source_target_pairs={{0,8},{8,0},{1,9},{9,1},{2,10},{10,2},{3,11},{11,3},{4,12},{12,4},... | collective-permute-start | bytes 786440 | tf_op jit(solution)/shard_map/ppermute | solution.py:18
  42.1 2.4 %collective-permute-start.11 = (bf16[1024,128]{1,0:T(8,128)(2,1)S(1)}, bf16[1024,128]{1,0:T(8,128)(2,1)S(1)}, u32[]{:S(2)}, u32[]{:S(2)}) collective-permute-start(bf16[1024,128]{1,0:T(8,128)(2,1)S(1)} %pad_maximum_fusion.5), channel_id=1, source_target_pairs={{0,8},{8,0},{1,9},{9,1},{2,10},{10,2},{3,11},{11,3},{4,12},{12,4},... | collective-permute-start | bytes 786440 | tf_op jit(solution)/shard_map/ppermute | solution.py:18
  44.5 0.0 collective-permute-done.9.refs_3_
  44.5 0.0 collective-permute-done.10.refs_4_
  44.6 2.6 %collective-permute-start.12 = (bf16[1024,128]{1,0:T(8,128)(2,1)S(1)}, bf16[1024,128]{1,0:T(8,128)(2,1)S(1)}, u32[]{:S(2)}, u32[]{:S(2)}) collective-permute-start(bf16[1024,128]{1,0:T(8,128)(2,1)S(1)} %pad_maximum_fusion.6), channel_id=1, source_target_pairs={{0,8},{8,0},{1,9},{9,1},{2,10},{10,2},{3,11},{11,3},{4,12},{12,4},... | collective-permute-start | bytes 786440 | tf_op jit(solution)/shard_map/ppermute | solution.py:18
  47.9 0.0 copy-done.1
  47.9 5.2 %prepare.1 = (f32[16512,128]{1,0:T(8,128)S(1)}, s32[975]{0:T(1024)S(1)}, bf16[320,128,128]{2,1,0:T(8,128)(2,1)S(1)}) custom-call(s32[1,1]{1,0:T(1,128)S(6)} %copy.16.refs_0_, s32[1,1,320]{2,1,0:T(1,128)S(1)} %copy-done.1, s32[1,1,320]{2,1,0:T(1,128)S(1)} %copy-done.2, bf16[1,1,320,128,128]{4,3,2,1,0:T(8,128)(2,1)} %refs_3_.1), custom_call_target="tpu_custom_call" | custom-call | tf_op jit(solution)/shard_map/prepare/pallas_call | solution.py:138
  53.1 0.0 collective-permute-done.3.refs_4_
  53.1 1.3 %shard_map.91.acc_in = f32[16512,128]{1,0:T(8,128)S(1)} custom-call(s32[975]{0:T(1024)S(1)} %get-tuple-element.13.codes_ref, bf16[320,128,128]{2,1,0:T(8,128)(2,1)S(1)} %get-tuple-element.14.tiles_ref, f32[16512,128]{1,0:T(8,128)S(1)} %get-tuple-element.15.acc_in, ...), custom_call_target="tpu_custom_call", output_to_operand_aliasing={{}: (2, {})} | custom-call | tf_op jit(solution)/shard_map/pallas_call | solution.py:197
  54.4 0.3 collective-permute-done.6.refs_0_
  54.7 1.2 %shard_map.92.acc_in = f32[16512,128]{1,0:T(8,128)S(1)} custom-call(s32[975]{0:T(1024)S(1)} %get-tuple-element.13.codes_ref, bf16[320,128,128]{2,1,0:T(8,128)(2,1)S(1)} %get-tuple-element.14.tiles_ref, f32[16512,128]{1,0:T(8,128)S(1)} %shard_map.91.acc_in, bf16[1024,128]{1,0:T(8,128)(2,1)S(1)} %collective-permute-done.6.refs_0_, ...), custom_call_target="tpu_custom_call", output_to_operand_aliasing={{}: (2, {})} | custom-call | tf_op jit(solution)/shard_map/pallas_call | solution.py:197
  55.9 2.8 %collective-permute-done.11.refs_0_ = bf16[1024,128]{1,0:T(8,128)(2,1)S(1)} collective-permute-done((bf16[1024,128]{1,0:T(8,128)(2,1)S(1)}, bf16[1024,128]{1,0:T(8,128)(2,1)S(1)}, u32[]{:S(2)}, u32[]{:S(2)}) %collective-permute-start.11) | collective-permute-done | bytes 262176 | tf_op jit(solution)/shard_map/ppermute | solution.py:18
  58.7 2.8 %collective-permute-done.12.refs_1_ = bf16[1024,128]{1,0:T(8,128)(2,1)S(1)} collective-permute-done((bf16[1024,128]{1,0:T(8,128)(2,1)S(1)}, bf16[1024,128]{1,0:T(8,128)(2,1)S(1)}, u32[]{:S(2)}, u32[]{:S(2)}) %collective-permute-start.12) | collective-permute-done | bytes 262176 | tf_op jit(solution)/shard_map/ppermute | solution.py:18
  61.6 1.2 %shard_map.93 = (f32[16512,128]{1,0:T(8,128)S(1)}, bf16[8,688,128]{2,1,0:T(8,128)(2,1)S(1)}, bf16[8,688,128]{2,1,0:T(8,128)(2,1)S(1)}) custom-call(s32[975]{0:T(1024)S(1)} %get-tuple-element.13.codes_ref, bf16[320,128,128]{2,1,0:T(8,128)(2,1)S(1)} %get-tuple-element.14.tiles_ref, ...), custom_call_target="tpu_custom_call", output_to_operand_aliasing={{0}: (2, {})} | custom-call | tf_op jit(solution)/shard_map/pallas_call | solution.py:242
  62.8 0.1 collective-permute-start.13
  62.9 0.2 rest.1
  63.1 0.6 collective-permute-start.17
  63.6 2.4 %collective-permute-done.13 = bf16[8,688,128]{2,1,0:T(8,128)(2,1)S(1)} collective-permute-done((bf16[8,688,128]{2,1,0:T(8,128)(2,1)S(1)}, bf16[8,688,128]{2,1,0:T(8,128)(2,1)S(1)}, u32[]{:S(2)}, u32[]{:S(2)}) %collective-permute-start.13) | collective-permute-done | bytes 1409056 | tf_op jit(solution)/shard_map/ppermute | solution.py:18
  66.0 0.2 add_convert_fusion
  66.2 2.4 %collective-permute-start.14 = (bf16[4,688,128]{2,1,0:T(8,128)(2,1)S(1)}, bf16[4,688,128]{2,1,0:T(8,128)(2,1)S(1)}, u32[]{:S(2)}, u32[]{:S(2)}) collective-permute-start(bf16[4,688,128]{2,1,0:T(8,128)(2,1)S(1)} %add_convert_fusion), channel_id=1, source_target_pairs={{0,128},{16,48},{32,160},{48,16},{64,192},{80,112},{96,224},{112,8... | collective-permute-start | bytes 2113544 | tf_op jit(solution)/shard_map/ppermute | solution.py:275
  68.6 0.0 collective-permute-done.17
  68.6 0.1 add_convert_fusion.2
  68.7 3.2 %collective-permute-start.18 = (bf16[4,336,128]{2,1,0:T(8,128)(2,1)S(1)}, bf16[4,336,128]{2,1,0:T(8,128)(2,1)S(1)}, u32[]{:S(2)}, u32[]{:S(2)}) collective-permute-start(bf16[4,336,128]{2,1,0:T(8,128)(2,1)S(1)} %add_convert_fusion.2), channel_id=1, source_target_pairs={{0,96},{16,112},{32,64},{48,80},{64,32},{80,48},{96,0},{112,16},{1... | collective-permute-start | bytes 1032200 | tf_op jit(solution)/shard_map/ppermute | solution.py:275
  71.9 8.2 %collective-permute-done.18 = bf16[4,336,128]{2,1,0:T(8,128)(2,1)S(1)} collective-permute-done((bf16[4,336,128]{2,1,0:T(8,128)(2,1)S(1)}, bf16[4,336,128]{2,1,0:T(8,128)(2,1)S(1)}, u32[]{:S(2)}, u32[]{:S(2)}) %collective-permute-start.18) | collective-permute-done | bytes 344096 | tf_op jit(solution)/shard_map/ppermute | solution.py:275
  80.1 0.1 add_convert_fusion.4
  80.2 1.4 %collective-permute-start.19 = (bf16[2,336,128]{2,1,0:T(8,128)(2,1)S(1)}, bf16[2,336,128]{2,1,0:T(8,128)(2,1)S(1)}, u32[]{:S(2)}, u32[]{:S(2)}) collective-permute-start(bf16[2,336,128]{2,1,0:T(8,128)(2,1)S(1)} %add_convert_fusion.4), channel_id=1, source_target_pairs={{0,128},{16,144},{32,160},{48,176},{64,192},{80,208},{96,224},{112... | collective-permute-start | bytes 516104 | tf_op jit(solution)/shard_map/ppermute | solution.py:275
  81.6 0.0 collective-permute-done.14
  81.6 0.1 add_convert_fusion.1
  81.8 0.7 collective-permute-start.15
  82.5 3.9 %collective-permute-done.19 = bf16[2,336,128]{2,1,0:T(8,128)(2,1)S(1)} collective-permute-done((bf16[2,336,128]{2,1,0:T(8,128)(2,1)S(1)}, bf16[2,336,128]{2,1,0:T(8,128)(2,1)S(1)}, u32[]{:S(2)}, u32[]{:S(2)}) %collective-permute-start.19) | collective-permute-done | bytes 172064 | tf_op jit(solution)/shard_map/ppermute | solution.py:275
  86.4 0.1 add_convert_fusion.5
  86.4 0.0 copy-start.3
  86.5 0.0 copy-start.4
  86.5 0.1 collective-permute-start.20
  86.6 3.6 %collective-permute-done.15 = bf16[2,688,128]{2,1,0:T(8,128)(2,1)S(1)} collective-permute-done((bf16[2,688,128]{2,1,0:T(8,128)(2,1)S(1)}, bf16[2,688,128]{2,1,0:T(8,128)(2,1)S(1)}, u32[]{:S(2)}, u32[]{:S(2)}) %collective-permute-start.15) | collective-permute-done | bytes 352288 | tf_op jit(solution)/shard_map/ppermute | solution.py:275
  90.1 0.1 add_convert_fusion.3
  90.2 3.3 %collective-permute-start.16 = (bf16[1,688,128]{2,1,0:T(8,128)(2,1)S(1)}, bf16[1,688,128]{2,1,0:T(8,128)(2,1)S(1)}, u32[]{:S(2)}, u32[]{:S(2)}) collective-permute-start(bf16[1,688,128]{2,1,0:T(8,128)(2,1)S(1)} %add_convert_fusion.3), channel_id=1, source_target_pairs={{0,96},{16,144},{32,64},{48,176},{64,32},{80,208},{96,0},{112,240}... | collective-permute-start | bytes 528392 | tf_op jit(solution)/shard_map/ppermute | solution.py:275
  93.5 0.0 collective-permute-done.20
  93.5 0.1 add_bitcast_fusion.1
  93.6 3.4 %collective-permute-done.16 = bf16[1,688,128]{2,1,0:T(8,128)(2,1)S(1)} collective-permute-done((bf16[1,688,128]{2,1,0:T(8,128)(2,1)S(1)}, bf16[1,688,128]{2,1,0:T(8,128)(2,1)S(1)}, u32[]{:S(2)}, u32[]{:S(2)}) %collective-permute-start.16) | collective-permute-done | bytes 176160 | tf_op jit(solution)/shard_map/ppermute | solution.py:275
  97.0 0.1 add_bitcast_fusion
  97.1 1.0 %fusion.2 = bf16[1,1024,128]{2,1,0:T(8,128)(2,1)} fusion(bf16[128,128]{1,0:T(8,128)(2,1)S(1)} %copy-done, f32[336,128]{1,0:T(8,128)S(1)} %add_bitcast_fusion.1, f32[688,128]{1,0:T(8,128)S(1)} %add_bitcast_fusion, f32[128]{0:T(128)S(1)} %copy-done.4, f32[1024]{0:T(1024)S(1)} %bitcast.8), kind=kOutput, calls=%fused_computation.4 | convolution fusion | flops 34340864 | bytes 823808 | tf_op jit(solution)/shard_map/dot_general | solution.py:304
  (19 shorter events, 0.2 us)
Async XLA Ops:
  0.0 97.1 %copy-start = (bf16[128,128]{1,0:T(8,128)(2,1)S(1)}, bf16[128,128]{1,0:T(8,128)(2,1)}, u32[]{:S(2)}) copy-start(bf16[128,128]{1,0:T(8,128)(2,1)} %param.16) | copy-start | bytes 98308
  1.2 9.6 %collective-permute-start = (bf16[1024,128]{1,0:T(8,128)(2,1)S(1)}, bf16[1024,128]{1,0:T(8,128)(2,1)S(1)}, u32[]{:S(2)}, u32[]{:S(2)}) collective-permute-start(bf16[1024,128]{1,0:T(8,128)(2,1)S(1)} %multiply_convert_fusion.refs_0_), channel_id=1, source_target_pairs={{0,8},{8,0},{1,9},{9,1},{2,10},{10,2},{3,11},{11,3},{4,12},{12,4},... | collective-permute-start | bytes 786440 | tf_op jit(solution)/shard_map/ppermute | solution.py:18
  3.5 7.4 %collective-permute-start.1 = (bf16[1024,128]{1,0:T(8,128)(2,1)S(1)}, bf16[1024,128]{1,0:T(8,128)(2,1)S(1)}, u32[]{:S(2)}, u32[]{:S(2)}) collective-permute-start(bf16[1024,128]{1,0:T(8,128)(2,1)S(1)} %multiply_convert_fusion.refs_0_), channel_id=1, source_target_pairs={{0,1},{1,0},{2,3},{3,2},{4,5},{5,4},{6,7},{7,6},{8,9},{9,8},{10,11... | collective-permute-start | bytes 786440 | tf_op jit(solution)/shard_map/ppermute | solution.py:18
  3.7 10.7 %collective-permute-start.2 = (bf16[1024,128]{1,0:T(8,128)(2,1)S(1)}, bf16[1024,128]{1,0:T(8,128)(2,1)S(1)}, u32[]{:S(2)}, u32[]{:S(2)}) collective-permute-start(bf16[1024,128]{1,0:T(8,128)(2,1)S(1)} %multiply_convert_fusion.refs_0_), channel_id=1, source_target_pairs={{0,7},{1,2},{2,1},{3,4},{4,3},{5,6},{6,5},{7,0},{8,15},{9,10},{10,... | collective-permute-start | bytes 786440 | tf_op jit(solution)/shard_map/ppermute | solution.py:18
  14.4 9.8 %collective-permute-start.4 = (bf16[1536,128]{1,0:T(8,128)(2,1)S(1)}, bf16[1536,128]{1,0:T(8,128)(2,1)S(1)}, u32[]{:S(2)}, u32[]{:S(2)}) collective-permute-start(bf16[1536,128]{1,0:T(8,128)(2,1)S(1)} %get-tuple-element.25), channel_id=1, source_target_pairs={{0,1},{1,0},{2,3},{3,2},{4,5},{5,4},{6,7},{7,6},{8,9},{9,8},{10,11... | collective-permute-start | bytes 1179656 | tf_op jit(solution)/shard_map/ppermute | solution.py:18
  14.5 12.4 %collective-permute-start.5 = (bf16[1536,128]{1,0:T(8,128)(2,1)S(1)}, bf16[1536,128]{1,0:T(8,128)(2,1)S(1)}, u32[]{:S(2)}, u32[]{:S(2)}) collective-permute-start(bf16[1536,128]{1,0:T(8,128)(2,1)S(1)} %get-tuple-element.24), channel_id=1, source_target_pairs={{0,7},{1,2},{2,1},{3,4},{4,3},{5,6},{6,5},{7,0},{8,15},{9,10},{10,... | collective-permute-start | bytes 1179656 | tf_op jit(solution)/shard_map/ppermute | solution.py:18
  24.2 10.1 %collective-permute-start.8 = (bf16[1536,128]{1,0:T(8,128)(2,1)S(1)}, bf16[1536,128]{1,0:T(8,128)(2,1)S(1)}, u32[]{:S(2)}, u32[]{:S(2)}) collective-permute-start(bf16[1536,128]{1,0:T(8,128)(2,1)S(1)} %collective-permute-done.4.refs_5_), channel_id=1, source_target_pairs={{0,7},{1,2},{2,1},{3,4},{4,3},{5,6},{6,5},{7,0},{8,15},{9,10},{10,... | collective-permute-start | bytes 1179656 | tf_op jit(solution)/shard_map/ppermute | solution.py:18
  26.9 9.5 %collective-permute-start.7 = (bf16[1536,128]{1,0:T(8,128)(2,1)S(1)}, bf16[1536,128]{1,0:T(8,128)(2,1)S(1)}, u32[]{:S(2)}, u32[]{:S(2)}) collective-permute-start(bf16[1536,128]{1,0:T(8,128)(2,1)S(1)} %collective-permute-done.5.refs_6_), channel_id=1, source_target_pairs={{0,1},{1,0},{2,3},{3,2},{4,5},{5,4},{6,7},{7,6},{8,9},{9,8},{10,11... | collective-permute-start | bytes 1179656 | tf_op jit(solution)/shard_map/ppermute | solution.py:18
  34.4 10.2 %collective-permute-start.9 = (bf16[1024,128]{1,0:T(8,128)(2,1)S(1)}, bf16[1024,128]{1,0:T(8,128)(2,1)S(1)}, u32[]{:S(2)}, u32[]{:S(2)}) collective-permute-start(bf16[1024,128]{1,0:T(8,128)(2,1)S(1)} %pad_maximum_fusion.4), channel_id=1, source_target_pairs={{0,1},{1,0},{2,3},{3,2},{4,5},{5,4},{6,7},{7,6},{8,9},{9,8},{10,11... | collective-permute-start | bytes 786440 | tf_op jit(solution)/shard_map/ppermute | solution.py:18
  36.4 8.1 %collective-permute-start.10 = (bf16[1024,128]{1,0:T(8,128)(2,1)S(1)}, bf16[1024,128]{1,0:T(8,128)(2,1)S(1)}, u32[]{:S(2)}, u32[]{:S(2)}) collective-permute-start(bf16[1024,128]{1,0:T(8,128)(2,1)S(1)} %slice.189), channel_id=1, source_target_pairs={{0,7},{1,2},{2,1},{3,4},{4,3},{5,6},{6,5},{7,0},{8,15},{9,10},{10,... | collective-permute-start | bytes 786440 | tf_op jit(solution)/shard_map/ppermute | solution.py:18
  38.3 9.6 %copy-start.1 = (s32[1,1,320]{2,1,0:T(1,128)S(1)}, s32[1,1,320]{2,1,0:T(1,128)}, u32[]{:S(2)}) copy-start(s32[1,1,320]{2,1,0:T(1,128)} %refs_1_.1) | copy-start | bytes 3844
  38.3 9.6 %copy-start.2 = (s32[1,1,320]{2,1,0:T(1,128)S(1)}, s32[1,1,320]{2,1,0:T(1,128)}, u32[]{:S(2)}) copy-start(s32[1,1,320]{2,1,0:T(1,128)} %refs_2_.1) | copy-start | bytes 3844
  38.3 14.8 %collective-permute-start.3 = (bf16[1024,128]{1,0:T(8,128)(2,1)S(1)}, bf16[1024,128]{1,0:T(8,128)(2,1)S(1)}, u32[]{:S(2)}, u32[]{:S(2)}) collective-permute-start(bf16[1024,128]{1,0:T(8,128)(2,1)S(1)} %pad_maximum_fusion.2), channel_id=1, source_target_pairs={{0,8},{8,0},{1,9},{9,1},{2,10},{10,2},{3,11},{11,3},{4,12},{12,4},... | collective-permute-start | bytes 786440 | tf_op jit(solution)/shard_map/ppermute | solution.py:18
  40.8 13.9 %collective-permute-start.6 = (bf16[1024,128]{1,0:T(8,128)(2,1)S(1)}, bf16[1024,128]{1,0:T(8,128)(2,1)S(1)}, u32[]{:S(2)}, u32[]{:S(2)}) collective-permute-start(bf16[1024,128]{1,0:T(8,128)(2,1)S(1)} %pad_maximum_fusion.3), channel_id=1, source_target_pairs={{0,8},{8,0},{1,9},{9,1},{2,10},{10,2},{3,11},{11,3},{4,12},{12,4},... | collective-permute-start | bytes 786440 | tf_op jit(solution)/shard_map/ppermute | solution.py:18
  42.1 16.7 %collective-permute-start.11 = (bf16[1024,128]{1,0:T(8,128)(2,1)S(1)}, bf16[1024,128]{1,0:T(8,128)(2,1)S(1)}, u32[]{:S(2)}, u32[]{:S(2)}) collective-permute-start(bf16[1024,128]{1,0:T(8,128)(2,1)S(1)} %pad_maximum_fusion.5), channel_id=1, source_target_pairs={{0,8},{8,0},{1,9},{9,1},{2,10},{10,2},{3,11},{11,3},{4,12},{12,4},... | collective-permute-start | bytes 786440 | tf_op jit(solution)/shard_map/ppermute | solution.py:18
  44.6 17.0 %collective-permute-start.12 = (bf16[1024,128]{1,0:T(8,128)(2,1)S(1)}, bf16[1024,128]{1,0:T(8,128)(2,1)S(1)}, u32[]{:S(2)}, u32[]{:S(2)}) collective-permute-start(bf16[1024,128]{1,0:T(8,128)(2,1)S(1)} %pad_maximum_fusion.6), channel_id=1, source_target_pairs={{0,8},{8,0},{1,9},{9,1},{2,10},{10,2},{3,11},{11,3},{4,12},{12,4},... | collective-permute-start | bytes 786440 | tf_op jit(solution)/shard_map/ppermute | solution.py:18
  62.8 3.3 %collective-permute-start.13 = (bf16[8,688,128]{2,1,0:T(8,128)(2,1)S(1)}, bf16[8,688,128]{2,1,0:T(8,128)(2,1)S(1)}, u32[]{:S(2)}, u32[]{:S(2)}) collective-permute-start(bf16[8,688,128]{2,1,0:T(8,128)(2,1)S(1)} %get-tuple-element.17), channel_id=1, source_target_pairs={{0,16},{16,0},{1,17},{17,1},{2,18},{18,2},{3,19},{19,3},{4,20},{20... | collective-permute-start | bytes 4227080 | tf_op jit(solution)/shard_map/ppermute | solution.py:18
  63.1 5.6 %collective-permute-start.17 = (bf16[8,336,128]{2,1,0:T(8,128)(2,1)S(1)}, bf16[8,336,128]{2,1,0:T(8,128)(2,1)S(1)}, u32[]{:S(2)}, u32[]{:S(2)}) collective-permute-start(bf16[8,336,128]{2,1,0:T(8,128)(2,1)S(1)} %get-tuple-element.20), channel_id=1, source_target_pairs={{0,16},{16,0},{1,17},{17,1},{2,18},{18,2},{3,19},{19,3},{4,20},{20... | collective-permute-start | bytes 2064392 | tf_op jit(solution)/shard_map/ppermute | solution.py:18
  66.2 15.4 %collective-permute-start.14 = (bf16[4,688,128]{2,1,0:T(8,128)(2,1)S(1)}, bf16[4,688,128]{2,1,0:T(8,128)(2,1)S(1)}, u32[]{:S(2)}, u32[]{:S(2)}) collective-permute-start(bf16[4,688,128]{2,1,0:T(8,128)(2,1)S(1)} %add_convert_fusion), channel_id=1, source_target_pairs={{0,128},{16,48},{32,160},{48,16},{64,192},{80,112},{96,224},{112,8... | collective-permute-start | bytes 2113544 | tf_op jit(solution)/shard_map/ppermute | solution.py:275
  68.7 11.4 %collective-permute-start.18 = (bf16[4,336,128]{2,1,0:T(8,128)(2,1)S(1)}, bf16[4,336,128]{2,1,0:T(8,128)(2,1)S(1)}, u32[]{:S(2)}, u32[]{:S(2)}) collective-permute-start(bf16[4,336,128]{2,1,0:T(8,128)(2,1)S(1)} %add_convert_fusion.2), channel_id=1, source_target_pairs={{0,96},{16,112},{32,64},{48,80},{64,32},{80,48},{96,0},{112,16},{1... | collective-permute-start | bytes 1032200 | tf_op jit(solution)/shard_map/ppermute | solution.py:275
  80.2 6.2 %collective-permute-start.19 = (bf16[2,336,128]{2,1,0:T(8,128)(2,1)S(1)}, bf16[2,336,128]{2,1,0:T(8,128)(2,1)S(1)}, u32[]{:S(2)}, u32[]{:S(2)}) collective-permute-start(bf16[2,336,128]{2,1,0:T(8,128)(2,1)S(1)} %add_convert_fusion.4), channel_id=1, source_target_pairs={{0,128},{16,144},{32,160},{48,176},{64,192},{80,208},{96,224},{112... | collective-permute-start | bytes 516104 | tf_op jit(solution)/shard_map/ppermute | solution.py:275
  81.8 8.3 %collective-permute-start.15 = (bf16[2,688,128]{2,1,0:T(8,128)(2,1)S(1)}, bf16[2,688,128]{2,1,0:T(8,128)(2,1)S(1)}, u32[]{:S(2)}, u32[]{:S(2)}) collective-permute-start(bf16[2,688,128]{2,1,0:T(8,128)(2,1)S(1)} %add_convert_fusion.1), channel_id=1, source_target_pairs={{0,32},{16,112},{32,0},{48,80},{64,96},{80,48},{96,64},{112,16},{1... | collective-permute-start | bytes 1056776 | tf_op jit(solution)/shard_map/ppermute | solution.py:275
  86.4 10.7 %copy-start.3 = (f32[1,1024]{1,0:T(1,128)S(1)}, f32[1,1024]{1,0:T(1,128)}, u32[]{:S(2)}) copy-start(f32[1,1024]{1,0:T(1,128)} %param.11) | copy-start | bytes 12292
  86.5 10.7 %copy-start.4 = (f32[128]{0:T(128)S(1)}, f32[128]{0:T(128)}, u32[]{:S(2)}) copy-start(f32[128]{0:T(128)} %param.17) | copy-start | bytes 1540
  86.5 7.1 %collective-permute-start.20 = (bf16[1,336,128]{2,1,0:T(8,128)(2,1)S(1)}, bf16[1,336,128]{2,1,0:T(8,128)(2,1)S(1)}, u32[]{:S(2)}, u32[]{:S(2)}) collective-permute-start(bf16[1,336,128]{2,1,0:T(8,128)(2,1)S(1)} %add_convert_fusion.5), channel_id=1, source_target_pairs={{0,32},{16,48},{32,0},{48,16},{64,96},{80,112},{96,64},{112,80},{1... | collective-permute-start | bytes 258056 | tf_op jit(solution)/shard_map/ppermute | solution.py:275
  90.2 6.7 %collective-permute-start.16 = (bf16[1,688,128]{2,1,0:T(8,128)(2,1)S(1)}, bf16[1,688,128]{2,1,0:T(8,128)(2,1)S(1)}, u32[]{:S(2)}, u32[]{:S(2)}) collective-permute-start(bf16[1,688,128]{2,1,0:T(8,128)(2,1)S(1)} %add_convert_fusion.3), channel_id=1, source_target_pairs={{0,96},{16,144},{32,64},{48,176},{64,32},{80,208},{96,0},{112,240}... | collective-permute-start | bytes 528392 | tf_op jit(solution)/shard_map/ppermute | solution.py:275

commit v4 on v3

--- a/solution.py
+++ b/solution.py
@@ -26,15 +26,36 @@
     return i + (i & 1) * 2 - 1
 
 
+def copied(*pieces):
+    width = pieces[0][0].shape[1]
+    total = sum(rows for _, _, rows in pieces)
+
+    def kernel(*refs):
+        to = 0
+        for ref, (_, first, rows) in zip(refs, pieces):
+            refs[-1][to : to + rows] = ref[first : first + rows]
+            to += rows
+
+    vmem = pl.BlockSpec(memory_space=pltpu.VMEM)
+    return pl.pallas_call(
+        kernel,
+        out_shape=jax.ShapeDtypeStruct((total, width), BF16),
+        in_specs=[vmem] * len(pieces),
+        out_specs=vmem,
+        compiler_params=pltpu.CompilerParams(vmem_limit_bytes=4 * 2**20),
+        name="copied",
+    )(*(value for value, _, _ in pieces))
+
+
 def gathered(own):
     half = own.shape[0] // 2
     found = {(0, 0, 0): (own, 0), (0, 0, 1): (own, half)}
-    across = swapped(own, "xh", other)
     near = swapped(own, "z", other)
     back = swapped(own, "z", other_side)
-    other_top = across[:half]
-    found[1, 0, 0] = (across, 0)
-    found[1, 0, 1] = (across, half)
+    other_top = swapped(copied((own, 0, half)), "xh", other)
+    other_low = swapped(copied((own, half, half)), "xh", other)
+    found[1, 0, 0] = (other_top, 0)
+    found[1, 0, 1] = (other_low, 0)
     for step in (1, 2, 3):
         for sign, value in ((1, near), (-1, back)):
             found[0, sign * step, 0] = (value, 0)
@@ -49,7 +70,7 @@
         else:
             from_near = near[half:]
             from_back = jnp.concatenate([back[:half], back[2 * half :]])
-        lows = jnp.concatenate([near[half : 2 * half], back[half : 2 * half]])
+        lows = copied((near, half, half), (back, half, half))
         near = swapped(from_back, "z", other)
         back = swapped(from_near, "z", other_side)
         lows = swapped(lows, "xh", other)
@@ -59,7 +80,7 @@
     found[0, 4, 1] = (back, 0)
     found[1, 3, 0] = (near, half)
     found[1, -3, 0] = (back, half)
-    last = swapped(jnp.concatenate([near[:half], back[:half]]), "xh", other)
+    last = swapped(copied((near, 0, half), (back, 0, half)), "xh", other)
     found[1, 4, 0] = (last, 0)
     found[1, 4, 1] = (last, half)
     return found
@@ -69,8 +90,8 @@
 BLOCK = 16
 STEP = 4
 CAP = 320 + STEP
-SHARES = (688, 336)
-HALVINGS = ((("xl", 1, 3), (1, 3, "xl")), ((3, "xl", 1), (3, "xl", 1)))
+SHARES = (384, 640)
+HALVINGS = (((3, "xl", 1), (3, "xl", 1)), ((1, 3, "xl"), ("xl", 1, 3)))
 
 
 def phase_of(key):
@@ -279,10 +300,10 @@
     held = [[keep_a, swapped(send_a, "core", other)], [keep_b, swapped(send_b, "core", other)]]
     for step in range(3):
         size = 4 >> step
-        came = [
-            halved(added(*(v[size:] for v in values)).astype(BF16), part, step)
-            for part, values in enumerate(held)
-        ]
+        came = []
+        for part, values in enumerate(held):
+            leaving = added(*(v[size:] for v in values)).astype(BF16)
+            came.append(halved(leaving, part, step))
         held = [[v[:size] for v in values] + [new] for values, new in zip(held, came)]
     return jnp.concatenate([added(*values)[0] for values in held])
 

time: 99.3 us -> 106 us (1.067)
  waiting for transfers between devices: 48.6 us -> 53.6 us
  starting transfers between devices: 36.1 us -> 38 us
    ppermute x15 -> x16, waiting for transfers between devices: 29.6 us -> 38.1 us  [swapped(): return lax.ppermute(value, axis, [(i, partner(i) % n) for i in range(n)])]
    ppermute x6, starting transfers between devices: 11.1 us -> 16 us  [halved(): return lax.ppermute(value, ROW, [(i, partner(i)) for i in range(16)])]
    ppermute x6, waiting for transfers between devices: 19 us -> 15.5 us  [halved(): return lax.ppermute(value, ROW, [(i, partner(i)) for i in range(16)])]
    ppermute x15 -> x16, starting transfers between devices: 25 us -> 22 us  [swapped(): return lax.ppermute(value, axis, [(i, partner(i) % n) for i in range(n)])]
  transfers between devices with their start and end apart: 21 -> 22, of which waited for: 13 -> 12; matrix products, arithmetic and copies ran while one was open for 1% -> 1% of each run, Pallas kernels for 8% -> 7%
where the time goes in v4:
time: 106 us; the launch traced here: 105 us
  waiting for transfers between devices  53.6 us (51%)
  starting transfers between devices  38 us (36%)
  Pallas kernels  9.24 us (9%)
  other arithmetic  2.04 us (2%)
    ppermute x16, waiting for transfers between devices, swapped(): return lax.ppermute(value, axis, [(i, partner(i) % n) for i in range(n)])  38.1 us
    ppermute x16, starting transfers between devices, swapped(): return lax.ppermute(value, axis, [(i, partner(i) % n) for i in range(n)])  22 us
    ppermute x6, starting transfers between devices, halved(): return lax.ppermute(value, ROW, [(i, partner(i)) for i in range(16)])  16 us
    ppermute x6, waiting for transfers between devices, halved(): return lax.ppermute(value, ROW, [(i, partner(i)) for i in range(16)])  15.5 us
    pallas_call x1, Pallas kernels, prepared(): pl.pallas_call(kernel, out_shape=(jax.ShapeDtypeStruct(((dests + 1) * sid...  5.22 us
    pallas_call x2, Pallas kernels, phase_sums(): pl.pallas_call(kernel, out_shape=jax.ShapeDtypeStruct(acc.shape, acc.dtyp...  2.51 us
  transfers between devices with their start and end apart: 22, of which 12 were waited for; matrix products, arithmetic and copies ran while one was open for 1% of the time, Pallas kernels for 7%

profile of v4, /device:TPU:4, one launch (start us, length us, event | category | flops | bytes accessed | tf_op | source)
XLA Modules:
  0.0 104.9 jit_solution(15389456216099013956)
XLA Ops:
  0.0 1.2 %multiply_convert_fusion.refs_0_ = bf16[1024,128]{1,0:T(8,128)(2,1)S(1)} fusion(bf16[1024,128]{1,0:T(8,128)(2,1)} %param.9, f32[1024]{0:T(1024)} %param.10), kind=kLoop, calls=%fused_computation.9 | loop fusion | flops 393216 | bytes 528384 | tf_op jit(solution)/shard_map/convert_element_type | solution.py:314
  1.2 2.0 %collective-permute-start.2 = (bf16[1024,128]{1,0:T(8,128)(2,1)S(1)}, bf16[1024,128]{1,0:T(8,128)(2,1)S(1)}, u32[]{:S(2)}, u32[]{:S(2)}) collective-permute-start(bf16[1024,128]{1,0:T(8,128)(2,1)S(1)} %multiply_convert_fusion.refs_0_), channel_id=1, source_target_pairs={{0,1},{1,0},{2,3},{3,2},{4,5},{5,4},{6,7},{7,6},{8,9},{9,8},{10,11... | collective-permute-start | bytes 786440 | tf_op jit(solution)/shard_map/ppermute | solution.py:18
  3.2 4.9 %collective-permute-start.3 = (bf16[1024,128]{1,0:T(8,128)(2,1)S(1)}, bf16[1024,128]{1,0:T(8,128)(2,1)S(1)}, u32[]{:S(2)}, u32[]{:S(2)}) collective-permute-start(bf16[1024,128]{1,0:T(8,128)(2,1)S(1)} %multiply_convert_fusion.refs_0_), channel_id=1, source_target_pairs={{0,7},{1,2},{2,1},{3,4},{4,3},{5,6},{6,5},{7,0},{8,15},{9,10},{10,... | collective-permute-start | bytes 786440 | tf_op jit(solution)/shard_map/ppermute | solution.py:18
  8.1 0.6 collective-permute-start
  8.7 6.0 %collective-permute-done.refs_1_ = bf16[512,128]{1,0:T(8,128)(2,1)S(1)} collective-permute-done((bf16[512,128]{1,0:T(8,128)(2,1)S(1)}, bf16[512,128]{1,0:T(8,128)(2,1)S(1)}, u32[]{:S(2)}, u32[]{:S(2)}) %collective-permute-start) | collective-permute-done | bytes 131104 | tf_op jit(solution)/shard_map/ppermute | solution.py:18
  14.7 0.0 collective-permute-done.2.refs_0_.refs_3_
  14.7 0.0 collective-permute-done.3.refs_1_.refs_4_
  14.7 0.1 pad_maximum_fusion
  14.8 0.1 collective-permute-start.5
  14.9 2.5 %collective-permute-start.6 = (bf16[1536,128]{1,0:T(8,128)(2,1)S(1)}, bf16[1536,128]{1,0:T(8,128)(2,1)S(1)}, u32[]{:S(2)}, u32[]{:S(2)}) collective-permute-start(bf16[1536,128]{1,0:T(8,128)(2,1)S(1)} %get-tuple-element.23), channel_id=1, source_target_pairs={{0,7},{1,2},{2,1},{3,4},{4,3},{5,6},{6,5},{7,0},{8,15},{9,10},{10,... | collective-permute-start | bytes 1179656 | tf_op jit(solution)/shard_map/ppermute | solution.py:18
  17.3 6.9 %collective-permute-done.5.refs_6_.refs_0_ = bf16[1536,128]{1,0:T(8,128)(2,1)S(1)} collective-permute-done((bf16[1536,128]{1,0:T(8,128)(2,1)S(1)}, bf16[1536,128]{1,0:T(8,128)(2,1)S(1)}, u32[]{:S(2)}, u32[]{:S(2)}) %collective-permute-start.5) | collective-permute-done | bytes 393248 | tf_op jit(solution)/shard_map/ppermute | solution.py:18
  24.3 2.7 %collective-permute-start.9 = (bf16[1536,128]{1,0:T(8,128)(2,1)S(1)}, bf16[1536,128]{1,0:T(8,128)(2,1)S(1)}, u32[]{:S(2)}, u32[]{:S(2)}) collective-permute-start(bf16[1536,128]{1,0:T(8,128)(2,1)S(1)} %collective-permute-done.5.refs_6_.refs_0_), channel_id=1, source_target_pairs={{0,7},{1,2},{2,1},{3,4},{4,3},{5,6},{6,5},{7,0},{8,15},{9,10},{10,... | collective-permute-start | bytes 1179656 | tf_op jit(solution)/shard_map/ppermute | solution.py:18
  27.0 0.0 collective-permute-done.6.refs_7_.refs_1_
  27.0 0.1 collective-permute-start.8
  27.1 7.0 %collective-permute-done.9.refs_2_.refs_1_ = bf16[1536,128]{1,0:T(8,128)(2,1)S(1)} collective-permute-done((bf16[1536,128]{1,0:T(8,128)(2,1)S(1)}, bf16[1536,128]{1,0:T(8,128)(2,1)S(1)}, u32[]{:S(2)}, u32[]{:S(2)}) %collective-permute-start.9) | collective-permute-done | bytes 393248 | tf_op jit(solution)/shard_map/ppermute | solution.py:18
  34.1 0.5 collective-permute-start.10
  34.6 3.0 %collective-permute-done.8.refs_1_.refs_0_ = bf16[1536,128]{1,0:T(8,128)(2,1)S(1)} collective-permute-done((bf16[1536,128]{1,0:T(8,128)(2,1)S(1)}, bf16[1536,128]{1,0:T(8,128)(2,1)S(1)}, u32[]{:S(2)}, u32[]{:S(2)}) %collective-permute-start.8) | collective-permute-done | bytes 393248 | tf_op jit(solution)/shard_map/ppermute | solution.py:18
  37.6 0.1 collective-permute-start.11
  37.7 0.6 collective-permute-start.4
  38.3 0.0 copy-start.1
  38.3 0.0 copy-start.2
  38.4 3.1 %collective-permute-start.7 = (bf16[1024,128]{1,0:T(8,128)(2,1)S(1)}, bf16[1024,128]{1,0:T(8,128)(2,1)S(1)}, u32[]{:S(2)}, u32[]{:S(2)}) collective-permute-start(bf16[1024,128]{1,0:T(8,128)(2,1)S(1)} %copied.9), channel_id=1, source_target_pairs={{0,8},{8,0},{1,9},{9,1},{2,10},{10,2},{3,11},{11,3},{4,12},{12,4},... | collective-permute-start | bytes 786440 | tf_op jit(solution)/shard_map/ppermute | solution.py:18
  41.5 0.6 collective-permute-start.12
  42.1 0.0 collective-permute-done.10.refs_3_.refs_0_
  42.1 3.2 %collective-permute-done.11.refs_4_.refs_1_ = bf16[1024,128]{1,0:T(8,128)(2,1)S(1)} collective-permute-done((bf16[1024,128]{1,0:T(8,128)(2,1)S(1)}, bf16[1024,128]{1,0:T(8,128)(2,1)S(1)}, u32[]{:S(2)}, u32[]{:S(2)}) %collective-permute-start.11) | collective-permute-done | bytes 262176 | tf_op jit(solution)/shard_map/ppermute | solution.py:18
  45.3 0.6 collective-permute-start.13
  45.9 3.1 %collective-permute-start.1 = (bf16[512,128]{1,0:T(8,128)(2,1)S(1)}, bf16[512,128]{1,0:T(8,128)(2,1)S(1)}, u32[]{:S(2)}, u32[]{:S(2)}) collective-permute-start(bf16[512,128]{1,0:T(8,128)(2,1)S(1)} %copied.7), channel_id=1, source_target_pairs={{0,8},{8,0},{1,9},{9,1},{2,10},{10,2},{3,11},{11,3},{4,12},{12,4},... | collective-permute-start | bytes 393224 | tf_op jit(solution)/shard_map/ppermute | solution.py:18
  49.7 5.2 %prepare.1 = (f32[16512,128]{1,0:T(8,128)S(1)}, s32[975]{0:T(1024)S(1)}, bf16[320,128,128]{2,1,0:T(8,128)(2,1)S(1)}) custom-call(s32[1,1]{1,0:T(1,128)S(6)} %copy.16.refs_0_, s32[1,1,320]{2,1,0:T(1,128)S(1)} %copy-done.1, s32[1,1,320]{2,1,0:T(1,128)S(1)} %copy-done.2, bf16[1,1,320,128,128]{4,3,2,1,0:T(8,128)(2,1)} %refs_3_.1), custom_call_target="tpu_custom_call" | custom-call | tf_op jit(solution)/shard_map/prepare/pallas_call | solution.py:159
  54.9 9.4 %collective-permute-done.1.refs_2_ = bf16[512,128]{1,0:T(8,128)(2,1)S(1)} collective-permute-done((bf16[512,128]{1,0:T(8,128)(2,1)S(1)}, bf16[512,128]{1,0:T(8,128)(2,1)S(1)}, u32[]{:S(2)}, u32[]{:S(2)}) %collective-permute-start.1) | collective-permute-done | bytes 131104 | tf_op jit(solution)/shard_map/ppermute | solution.py:18
  64.3 0.0 collective-permute-done.4.refs_5_
  64.3 1.3 %shard_map.91.acc_in = f32[16512,128]{1,0:T(8,128)S(1)} custom-call(s32[975]{0:T(1024)S(1)} %get-tuple-element.13.codes_ref, bf16[320,128,128]{2,1,0:T(8,128)(2,1)S(1)} %get-tuple-element.14.tiles_ref, f32[16512,128]{1,0:T(8,128)S(1)} %get-tuple-element.15.acc_in, ...), custom_call_target="tpu_custom_call", output_to_operand_aliasing={{}: (2, {})} | custom-call | tf_op jit(solution)/shard_map/pallas_call | solution.py:218
  65.6 0.0 collective-permute-done.7.refs_0_
  65.6 1.2 %shard_map.92.acc_in = f32[16512,128]{1,0:T(8,128)S(1)} custom-call(s32[975]{0:T(1024)S(1)} %get-tuple-element.13.codes_ref, bf16[320,128,128]{2,1,0:T(8,128)(2,1)S(1)} %get-tuple-element.14.tiles_ref, f32[16512,128]{1,0:T(8,128)S(1)} %shard_map.91.acc_in, bf16[1024,128]{1,0:T(8,128)(2,1)S(1)} %collective-permute-done.7.refs_0_, ...), custom_call_target="tpu_custom_call", output_to_operand_aliasing={{}: (2, {})} | custom-call | tf_op jit(solution)/shard_map/pallas_call | solution.py:218
  66.8 0.0 collective-permute-done.12.refs_0_
  66.9 0.0 collective-permute-done.13.refs_1_
  66.9 1.1 %shard_map.93 = (f32[16512,128]{1,0:T(8,128)S(1)}, bf16[8,384,128]{2,1,0:T(8,128)(2,1)S(1)}, bf16[8,384,128]{2,1,0:T(8,128)(2,1)S(1)}) custom-call(s32[975]{0:T(1024)S(1)} %get-tuple-element.13.codes_ref, bf16[320,128,128]{2,1,0:T(8,128)(2,1)S(1)} %get-tuple-element.14.tiles_ref, ...), custom_call_target="tpu_custom_call", output_to_operand_aliasing={{0}: (2, {})} | custom-call | tf_op jit(solution)/shard_map/pallas_call | solution.py:263
  68.0 0.3 rest.1
  68.3 0.1 collective-permute-start.18
  68.4 0.5 collective-permute-start.14
  68.9 2.5 %collective-permute-done.18 = bf16[8,640,128]{2,1,0:T(8,128)(2,1)S(1)} collective-permute-done((bf16[8,640,128]{2,1,0:T(8,128)(2,1)S(1)}, bf16[8,640,128]{2,1,0:T(8,128)(2,1)S(1)}, u32[]{:S(2)}, u32[]{:S(2)}) %collective-permute-start.18) | collective-permute-done | bytes 1310752 | tf_op jit(solution)/shard_map/ppermute | solution.py:18
  71.4 0.2 add_convert_fusion
  71.6 7.3 %collective-permute-start.19 = (bf16[4,640,128]{2,1,0:T(8,128)(2,1)S(1)}, bf16[4,640,128]{2,1,0:T(8,128)(2,1)S(1)}, u32[]{:S(2)}, u32[]{:S(2)}) collective-permute-start(bf16[4,640,128]{2,1,0:T(8,128)(2,1)S(1)} %add_convert_fusion), channel_id=1, source_target_pairs={{0,32},{16,144},{32,0},{48,176},{64,96},{80,208},{96,64},{112,240}... | collective-permute-start | bytes 1966088 | tf_op jit(solution)/shard_map/ppermute | solution.py:296
  79.0 0.0 collective-permute-done.14
  79.0 0.1 add_convert_fusion.1
  79.1 0.3 collective-permute-start.15
  79.3 9.0 %collective-permute-done.15 = bf16[4,384,128]{2,1,0:T(8,128)(2,1)S(1)} collective-permute-done((bf16[4,384,128]{2,1,0:T(8,128)(2,1)S(1)}, bf16[4,384,128]{2,1,0:T(8,128)(2,1)S(1)}, u32[]{:S(2)}, u32[]{:S(2)}) %collective-permute-start.15) | collective-permute-done | bytes 393248 | tf_op jit(solution)/shard_map/ppermute | solution.py:296
  88.3 0.1 add_convert_fusion.3
  88.4 1.3 %collective-permute-start.16 = (bf16[2,384,128]{2,1,0:T(8,128)(2,1)S(1)}, bf16[2,384,128]{2,1,0:T(8,128)(2,1)S(1)}, u32[]{:S(2)}, u32[]{:S(2)}) collective-permute-start(bf16[2,384,128]{2,1,0:T(8,128)(2,1)S(1)} %add_convert_fusion.3), channel_id=1, source_target_pairs={{0,128},{16,144},{32,160},{48,176},{64,192},{80,208},{96,224},{112... | collective-permute-start | bytes 589832 | tf_op jit(solution)/shard_map/ppermute | solution.py:296
  89.7 0.0 collective-permute-done.19
  89.7 0.1 add_convert_fusion.2
  89.8 2.5 %collective-permute-start.20 = (bf16[2,640,128]{2,1,0:T(8,128)(2,1)S(1)}, bf16[2,640,128]{2,1,0:T(8,128)(2,1)S(1)}, u32[]{:S(2)}, u32[]{:S(2)}) collective-permute-start(bf16[2,640,128]{2,1,0:T(8,128)(2,1)S(1)} %add_convert_fusion.2), channel_id=1, source_target_pairs={{0,96},{16,48},{32,64},{48,16},{64,32},{80,112},{96,0},{112,80},{1... | collective-permute-start | bytes 983048 | tf_op jit(solution)/shard_map/ppermute | solution.py:296
  92.3 1.9 %collective-permute-done.16 = bf16[2,384,128]{2,1,0:T(8,128)(2,1)S(1)} collective-permute-done((bf16[2,384,128]{2,1,0:T(8,128)(2,1)S(1)}, bf16[2,384,128]{2,1,0:T(8,128)(2,1)S(1)}, u32[]{:S(2)}, u32[]{:S(2)}) %collective-permute-start.16) | collective-permute-done | bytes 196640 | tf_op jit(solution)/shard_map/ppermute | solution.py:296
  94.2 0.1 add_convert_fusion.5
  94.2 0.0 copy-start.3
  94.2 0.0 copy-start.4
  94.2 3.7 %collective-permute-start.17 = (bf16[1,384,128]{2,1,0:T(8,128)(2,1)S(1)}, bf16[1,384,128]{2,1,0:T(8,128)(2,1)S(1)}, u32[]{:S(2)}, u32[]{:S(2)}) collective-permute-start(bf16[1,384,128]{2,1,0:T(8,128)(2,1)S(1)} %add_convert_fusion.5), channel_id=1, source_target_pairs={{0,32},{16,48},{32,0},{48,16},{64,96},{80,112},{96,64},{112,80},{1... | collective-permute-start | bytes 294920 | tf_op jit(solution)/shard_map/ppermute | solution.py:296
  98.0 0.2 collective-permute-done.20
  98.2 0.1 add_convert_fusion.4
  98.3 0.9 collective-permute-start.21
  99.2 1.3 %collective-permute-done.17 = bf16[1,384,128]{2,1,0:T(8,128)(2,1)S(1)} collective-permute-done((bf16[1,384,128]{2,1,0:T(8,128)(2,1)S(1)}, bf16[1,384,128]{2,1,0:T(8,128)(2,1)S(1)}, u32[]{:S(2)}, u32[]{:S(2)}) %collective-permute-start.17) | collective-permute-done | bytes 98336 | tf_op jit(solution)/shard_map/ppermute | solution.py:296
  100.6 0.1 add_bitcast_fusion.1
  100.6 3.1 %collective-permute-done.21 = bf16[1,640,128]{2,1,0:T(8,128)(2,1)S(1)} collective-permute-done((bf16[1,640,128]{2,1,0:T(8,128)(2,1)S(1)}, bf16[1,640,128]{2,1,0:T(8,128)(2,1)S(1)}, u32[]{:S(2)}, u32[]{:S(2)}) %collective-permute-start.21) | collective-permute-done | bytes 163872 | tf_op jit(solution)/shard_map/ppermute | solution.py:296
  103.7 0.1 add_bitcast_fusion
  103.9 1.0 fusion.2
  (15 shorter events, 0.2 us)
Async XLA Ops:
  0.0 103.8 %copy-start = (bf16[128,128]{1,0:T(8,128)(2,1)S(1)}, bf16[128,128]{1,0:T(8,128)(2,1)}, u32[]{:S(2)}) copy-start(bf16[128,128]{1,0:T(8,128)(2,1)} %param.16) | copy-start | bytes 98308
  1.2 13.5 %collective-permute-start.2 = (bf16[1024,128]{1,0:T(8,128)(2,1)S(1)}, bf16[1024,128]{1,0:T(8,128)(2,1)S(1)}, u32[]{:S(2)}, u32[]{:S(2)}) collective-permute-start(bf16[1024,128]{1,0:T(8,128)(2,1)S(1)} %multiply_convert_fusion.refs_0_), channel_id=1, source_target_pairs={{0,1},{1,0},{2,3},{3,2},{4,5},{5,4},{6,7},{7,6},{8,9},{9,8},{10,11... | collective-permute-start | bytes 786440 | tf_op jit(solution)/shard_map/ppermute | solution.py:18
  3.2 11.5 %collective-permute-start.3 = (bf16[1024,128]{1,0:T(8,128)(2,1)S(1)}, bf16[1024,128]{1,0:T(8,128)(2,1)S(1)}, u32[]{:S(2)}, u32[]{:S(2)}) collective-permute-start(bf16[1024,128]{1,0:T(8,128)(2,1)S(1)} %multiply_convert_fusion.refs_0_), channel_id=1, source_target_pairs={{0,7},{1,2},{2,1},{3,4},{4,3},{5,6},{6,5},{7,0},{8,15},{9,10},{10,... | collective-permute-start | bytes 786440 | tf_op jit(solution)/shard_map/ppermute | solution.py:18
  8.1 6.6 %collective-permute-start = (bf16[512,128]{1,0:T(8,128)(2,1)S(1)}, bf16[512,128]{1,0:T(8,128)(2,1)S(1)}, u32[]{:S(2)}, u32[]{:S(2)}) collective-permute-start(bf16[512,128]{1,0:T(8,128)(2,1)S(1)} %copied.6), channel_id=1, source_target_pairs={{0,8},{8,0},{1,9},{9,1},{2,10},{10,2},{3,11},{11,3},{4,12},{12,4},... | collective-permute-start | bytes 393224 | tf_op jit(solution)/shard_map/ppermute | solution.py:18
  14.8 9.5 %collective-permute-start.5 = (bf16[1536,128]{1,0:T(8,128)(2,1)S(1)}, bf16[1536,128]{1,0:T(8,128)(2,1)S(1)}, u32[]{:S(2)}, u32[]{:S(2)}) collective-permute-start(bf16[1536,128]{1,0:T(8,128)(2,1)S(1)} %get-tuple-element.24), channel_id=1, source_target_pairs={{0,1},{1,0},{2,3},{3,2},{4,5},{5,4},{6,7},{7,6},{8,9},{9,8},{10,11... | collective-permute-start | bytes 1179656 | tf_op jit(solution)/shard_map/ppermute | solution.py:18
  14.9 12.1 %collective-permute-start.6 = (bf16[1536,128]{1,0:T(8,128)(2,1)S(1)}, bf16[1536,128]{1,0:T(8,128)(2,1)S(1)}, u32[]{:S(2)}, u32[]{:S(2)}) collective-permute-start(bf16[1536,128]{1,0:T(8,128)(2,1)S(1)} %get-tuple-element.23), channel_id=1, source_target_pairs={{0,7},{1,2},{2,1},{3,4},{4,3},{5,6},{6,5},{7,0},{8,15},{9,10},{10,... | collective-permute-start | bytes 1179656 | tf_op jit(solution)/shard_map/ppermute | solution.py:18
  24.3 9.8 %collective-permute-start.9 = (bf16[1536,128]{1,0:T(8,128)(2,1)S(1)}, bf16[1536,128]{1,0:T(8,128)(2,1)S(1)}, u32[]{:S(2)}, u32[]{:S(2)}) collective-permute-start(bf16[1536,128]{1,0:T(8,128)(2,1)S(1)} %collective-permute-done.5.refs_6_.refs_0_), channel_id=1, source_target_pairs={{0,7},{1,2},{2,1},{3,4},{4,3},{5,6},{6,5},{7,0},{8,15},{9,10},{10,... | collective-permute-start | bytes 1179656 | tf_op jit(solution)/shard_map/ppermute | solution.py:18
  27.0 10.6 %collective-permute-start.8 = (bf16[1536,128]{1,0:T(8,128)(2,1)S(1)}, bf16[1536,128]{1,0:T(8,128)(2,1)S(1)}, u32[]{:S(2)}, u32[]{:S(2)}) collective-permute-start(bf16[1536,128]{1,0:T(8,128)(2,1)S(1)} %collective-permute-done.6.refs_7_.refs_1_), channel_id=1, source_target_pairs={{0,1},{1,0},{2,3},{3,2},{4,5},{5,4},{6,7},{7,6},{8,9},{9,8},{10,11... | collective-permute-start | bytes 1179656 | tf_op jit(solution)/shard_map/ppermute | solution.py:18
  34.1 8.0 %collective-permute-start.10 = (bf16[1024,128]{1,0:T(8,128)(2,1)S(1)}, bf16[1024,128]{1,0:T(8,128)(2,1)S(1)}, u32[]{:S(2)}, u32[]{:S(2)}) collective-permute-start(bf16[1024,128]{1,0:T(8,128)(2,1)S(1)} %pad_maximum_fusion.2), channel_id=1, source_target_pairs={{0,1},{1,0},{2,3},{3,2},{4,5},{5,4},{6,7},{7,6},{8,9},{9,8},{10,11... | collective-permute-start | bytes 786440 | tf_op jit(solution)/shard_map/ppermute | solution.py:18
  37.6 7.7 %collective-permute-start.11 = (bf16[1024,128]{1,0:T(8,128)(2,1)S(1)}, bf16[1024,128]{1,0:T(8,128)(2,1)S(1)}, u32[]{:S(2)}, u32[]{:S(2)}) collective-permute-start(bf16[1024,128]{1,0:T(8,128)(2,1)S(1)} %slice.148), channel_id=1, source_target_pairs={{0,7},{1,2},{2,1},{3,4},{4,3},{5,6},{6,5},{7,0},{8,15},{9,10},{10,... | collective-permute-start | bytes 786440 | tf_op jit(solution)/shard_map/ppermute | solution.py:18
  37.7 26.6 %collective-permute-start.4 = (bf16[1024,128]{1,0:T(8,128)(2,1)S(1)}, bf16[1024,128]{1,0:T(8,128)(2,1)S(1)}, u32[]{:S(2)}, u32[]{:S(2)}) collective-permute-start(bf16[1024,128]{1,0:T(8,128)(2,1)S(1)} %copied.8), channel_id=1, source_target_pairs={{0,8},{8,0},{1,9},{9,1},{2,10},{10,2},{3,11},{11,3},{4,12},{12,4},... | collective-permute-start | bytes 786440 | tf_op jit(solution)/shard_map/ppermute | solution.py:18
  38.3 11.3 %copy-start.1 = (s32[1,1,320]{2,1,0:T(1,128)S(1)}, s32[1,1,320]{2,1,0:T(1,128)}, u32[]{:S(2)}) copy-start(s32[1,1,320]{2,1,0:T(1,128)} %refs_1_.1) | copy-start | bytes 3844
  38.3 11.3 %copy-start.2 = (s32[1,1,320]{2,1,0:T(1,128)S(1)}, s32[1,1,320]{2,1,0:T(1,128)}, u32[]{:S(2)}) copy-start(s32[1,1,320]{2,1,0:T(1,128)} %refs_2_.1) | copy-start | bytes 3844
  38.4 27.2 %collective-permute-start.7 = (bf16[1024,128]{1,0:T(8,128)(2,1)S(1)}, bf16[1024,128]{1,0:T(8,128)(2,1)S(1)}, u32[]{:S(2)}, u32[]{:S(2)}) collective-permute-start(bf16[1024,128]{1,0:T(8,128)(2,1)S(1)} %copied.9), channel_id=1, source_target_pairs={{0,8},{8,0},{1,9},{9,1},{2,10},{10,2},{3,11},{11,3},{4,12},{12,4},... | collective-permute-start | bytes 786440 | tf_op jit(solution)/shard_map/ppermute | solution.py:18
  41.5 25.4 %collective-permute-start.12 = (bf16[1024,128]{1,0:T(8,128)(2,1)S(1)}, bf16[1024,128]{1,0:T(8,128)(2,1)S(1)}, u32[]{:S(2)}, u32[]{:S(2)}) collective-permute-start(bf16[1024,128]{1,0:T(8,128)(2,1)S(1)} %copied.10), channel_id=1, source_target_pairs={{0,8},{8,0},{1,9},{9,1},{2,10},{10,2},{3,11},{11,3},{4,12},{12,4},... | collective-permute-start | bytes 786440 | tf_op jit(solution)/shard_map/ppermute | solution.py:18
  45.3 21.6 %collective-permute-start.13 = (bf16[1024,128]{1,0:T(8,128)(2,1)S(1)}, bf16[1024,128]{1,0:T(8,128)(2,1)S(1)}, u32[]{:S(2)}, u32[]{:S(2)}) collective-permute-start(bf16[1024,128]{1,0:T(8,128)(2,1)S(1)} %copied.11), channel_id=1, source_target_pairs={{0,8},{8,0},{1,9},{9,1},{2,10},{10,2},{3,11},{11,3},{4,12},{12,4},... | collective-permute-start | bytes 786440 | tf_op jit(solution)/shard_map/ppermute | solution.py:18
  45.9 18.4 %collective-permute-start.1 = (bf16[512,128]{1,0:T(8,128)(2,1)S(1)}, bf16[512,128]{1,0:T(8,128)(2,1)S(1)}, u32[]{:S(2)}, u32[]{:S(2)}) collective-permute-start(bf16[512,128]{1,0:T(8,128)(2,1)S(1)} %copied.7), channel_id=1, source_target_pairs={{0,8},{8,0},{1,9},{9,1},{2,10},{10,2},{3,11},{11,3},{4,12},{12,4},... | collective-permute-start | bytes 393224 | tf_op jit(solution)/shard_map/ppermute | solution.py:18
  68.3 3.1 %collective-permute-start.18 = (bf16[8,640,128]{2,1,0:T(8,128)(2,1)S(1)}, bf16[8,640,128]{2,1,0:T(8,128)(2,1)S(1)}, u32[]{:S(2)}, u32[]{:S(2)}) collective-permute-start(bf16[8,640,128]{2,1,0:T(8,128)(2,1)S(1)} %get-tuple-element.20), channel_id=1, source_target_pairs={{0,16},{16,0},{1,17},{17,1},{2,18},{18,2},{3,19},{19,3},{4,20},{20... | collective-permute-start | bytes 3932168 | tf_op jit(solution)/shard_map/ppermute | solution.py:18
  68.4 10.5 %collective-permute-start.14 = (bf16[8,384,128]{2,1,0:T(8,128)(2,1)S(1)}, bf16[8,384,128]{2,1,0:T(8,128)(2,1)S(1)}, u32[]{:S(2)}, u32[]{:S(2)}) collective-permute-start(bf16[8,384,128]{2,1,0:T(8,128)(2,1)S(1)} %get-tuple-element.17), channel_id=1, source_target_pairs={{0,16},{16,0},{1,17},{17,1},{2,18},{18,2},{3,19},{19,3},{4,20},{20... | collective-permute-start | bytes 2359304 | tf_op jit(solution)/shard_map/ppermute | solution.py:18
  71.6 18.1 %collective-permute-start.19 = (bf16[4,640,128]{2,1,0:T(8,128)(2,1)S(1)}, bf16[4,640,128]{2,1,0:T(8,128)(2,1)S(1)}, u32[]{:S(2)}, u32[]{:S(2)}) collective-permute-start(bf16[4,640,128]{2,1,0:T(8,128)(2,1)S(1)} %add_convert_fusion), channel_id=1, source_target_pairs={{0,32},{16,144},{32,0},{48,176},{64,96},{80,208},{96,64},{112,240}... | collective-permute-start | bytes 1966088 | tf_op jit(solution)/shard_map/ppermute | solution.py:296
  79.1 9.3 %collective-permute-start.15 = (bf16[4,384,128]{2,1,0:T(8,128)(2,1)S(1)}, bf16[4,384,128]{2,1,0:T(8,128)(2,1)S(1)}, u32[]{:S(2)}, u32[]{:S(2)}) collective-permute-start(bf16[4,384,128]{2,1,0:T(8,128)(2,1)S(1)} %add_convert_fusion.1), channel_id=1, source_target_pairs={{0,96},{16,112},{32,64},{48,80},{64,32},{80,48},{96,0},{112,16},{1... | collective-permute-start | bytes 1179656 | tf_op jit(solution)/shard_map/ppermute | solution.py:296
  88.4 5.8 %collective-permute-start.16 = (bf16[2,384,128]{2,1,0:T(8,128)(2,1)S(1)}, bf16[2,384,128]{2,1,0:T(8,128)(2,1)S(1)}, u32[]{:S(2)}, u32[]{:S(2)}) collective-permute-start(bf16[2,384,128]{2,1,0:T(8,128)(2,1)S(1)} %add_convert_fusion.3), channel_id=1, source_target_pairs={{0,128},{16,144},{32,160},{48,176},{64,192},{80,208},{96,224},{112... | collective-permute-start | bytes 589832 | tf_op jit(solution)/shard_map/ppermute | solution.py:296
  89.8 8.4 %collective-permute-start.20 = (bf16[2,640,128]{2,1,0:T(8,128)(2,1)S(1)}, bf16[2,640,128]{2,1,0:T(8,128)(2,1)S(1)}, u32[]{:S(2)}, u32[]{:S(2)}) collective-permute-start(bf16[2,640,128]{2,1,0:T(8,128)(2,1)S(1)} %add_convert_fusion.2), channel_id=1, source_target_pairs={{0,96},{16,48},{32,64},{48,16},{64,32},{80,112},{96,0},{112,80},{1... | collective-permute-start | bytes 983048 | tf_op jit(solution)/shard_map/ppermute | solution.py:296
  94.2 9.6 %copy-start.3 = (f32[1,1024]{1,0:T(1,128)S(1)}, f32[1,1024]{1,0:T(1,128)}, u32[]{:S(2)}) copy-start(f32[1,1024]{1,0:T(1,128)} %param.11) | copy-start | bytes 12292
  94.2 9.6 %copy-start.4 = (f32[128]{0:T(128)S(1)}, f32[128]{0:T(128)}, u32[]{:S(2)}) copy-start(f32[128]{0:T(128)} %param.17) | copy-start | bytes 1540
  94.2 6.3 %collective-permute-start.17 = (bf16[1,384,128]{2,1,0:T(8,128)(2,1)S(1)}, bf16[1,384,128]{2,1,0:T(8,128)(2,1)S(1)}, u32[]{:S(2)}, u32[]{:S(2)}) collective-permute-start(bf16[1,384,128]{2,1,0:T(8,128)(2,1)S(1)} %add_convert_fusion.5), channel_id=1, source_target_pairs={{0,32},{16,48},{32,0},{48,16},{64,96},{80,112},{96,64},{112,80},{1... | collective-permute-start | bytes 294920 | tf_op jit(solution)/shard_map/ppermute | solution.py:296
  98.3 5.4 %collective-permute-start.21 = (bf16[1,640,128]{2,1,0:T(8,128)(2,1)S(1)}, bf16[1,640,128]{2,1,0:T(8,128)(2,1)S(1)}, u32[]{:S(2)}, u32[]{:S(2)}) collective-permute-start(bf16[1,640,128]{2,1,0:T(8,128)(2,1)S(1)} %add_convert_fusion.4), channel_id=1, source_target_pairs={{0,128},{16,112},{32,160},{48,80},{64,192},{80,48},{96,224},{112,1... | collective-permute-start | bytes 491528 | tf_op jit(solution)/shard_map/ppermute | solution.py:296
